TPU v7x, 128 devices: a whole 4x4x4 slice. The times are simulated.
128 devices in a mesh: dp: 4 (over x), expert: 32 (over z, y, core).
Axes of the slice: x: 4, y: 4, z: 4, core: 2. Of those that a mesh axis runs over, the one named last changes fastest.
Arguments:
- master: float32 [2, 128, 64, 2880], P(None, 'expert', 'dp'), may hold values from -6 to 6
- moment_one: float32 [2, 128, 64, 2880], P(None, 'expert', 'dp'), may hold values from -1.2 to 1.2
- moment_two: float32 [2, 128, 64, 2880], P(None, 'expert', 'dp'), may hold values from 0.0005 to 0.5
- gradient: bfloat16 [2, 128, 64, 2880], P(None, 'expert', 'dp'), may hold values from -150000 to 150000
- old_slot: int32 [2, 128], replicated, may hold values from 0 to 127, as said below
- new_slot: int32 [2, 128], replicated, may hold values from 0 to 127, as said below
Outputs:
- new_master: float32 [2, 128, 64, 2880], P(None, 'expert', 'dp')
- new_moment_one: float32 [2, 128, 64, 2880], P(None, 'expert', 'dp')
- new_moment_two: float32 [2, 128, 64, 2880], P(None, 'expert', 'dp')
Inputs may be any that keep to these rules, and one draw needn't show every extreme that they name: `old_slot`: for each layer a permutation of 0 to 127; global slot s is held by index s // 4 of expert. `new_slot`: for each layer a permutation of 0 to 127; in each layer exactly 1 slot of each index of expert receives another expert than it held, and exactly 1 of the experts held by each index leaves its slot; all other experts keep their slot.
All inputs are finite; a program needn't handle non-finite values.
Results may differ from a plain program's by a relative error of at most 0.001.
Values sent between devices are 32-bit elements; how exact they have to be, the bound alone decides.
A program may use at most 64 MiB of HBM per device.

v0:
```python
import functools
import math

import jax
import jax.numpy as jnp
from jax import lax
from jax.sharding import Mesh
from jax.sharding import PartitionSpec as P

MOVE_DEV = 1
DP_EXPERT = ("dp", "expert_0", "expert_1", "expert_2")
EXPERT = ("expert_0", "expert_1", "expert_2")


BETA_ONE = 0.9
BETA_TWO = 0.95
LEARN_RATE = 0.05
DECAY_RATE = 0.1
ADAM_EPS = 1e-08
CLIP_RMS = 2.0
FIRST_FIX = 1.0 - 0.9**10
SECOND_FIX = 1.0 - 0.95**10


def by_axis(value, axes):
    return functools.reduce(lax.psum, axes, value)


def adam_update(master, moment_one, moment_two, gradient, clip_scale):
    scaled = gradient.astype(jnp.float32) * clip_scale
    first_moment = BETA_ONE * moment_one + (1.0 - BETA_ONE) * scaled
    second = BETA_TWO * moment_two + (1.0 - BETA_TWO) * scaled * scaled
    step_dir = first_moment / FIRST_FIX / (jnp.sqrt(second / SECOND_FIX) + ADAM_EPS)
    weights = master - LEARN_RATE * (step_dir + DECAY_RATE * master)
    return (weights, first_moment, second)


def clip_factor(square_sum, entry_count):
    return jnp.minimum(1.0, CLIP_RMS * math.sqrt(entry_count) / (jnp.sqrt(square_sum) + 1e-06))


def grad_total(gradient):
    widened = gradient.astype(jnp.float32)
    return by_axis(jnp.sum(widened * widened), DP_EXPERT)


def pick_rows(data, chosen):
    return jax.vmap(lambda layer_block, layer_pick: jnp.take(layer_block, layer_pick, axis=0))(
        data, chosen
    )


def build_plan(old_slot, new_slot, slot_count, group_size, my_index):
    layer_count = old_slot.shape[0]
    holder = jnp.argsort(new_slot, axis=1)
    resident = jnp.argsort(old_slot, axis=1)
    source = jnp.take_along_axis(old_slot, holder, axis=1)
    target = jnp.take_along_axis(new_slot, resident, axis=1)
    position = lax.broadcasted_iota(jnp.int32, source.shape, 1)
    leaving = target != position
    arriving = source != position
    capacity = MOVE_DEV
    shaped = (layer_count, group_size, slot_count)
    out_order = jnp.argsort(jnp.where(leaving, 0, 1).reshape(shaped), axis=2, stable=True)[
        :, :, :capacity
    ]
    in_order = jnp.argsort(jnp.where(arriving, 0, 1).reshape(shaped), axis=2, stable=True)[
        :, :, :capacity
    ]
    out_rank = (jnp.cumsum(leaving.astype(jnp.int32).reshape(shaped), axis=2) - 1).reshape(
        source.shape
    )
    in_rank = jnp.cumsum(arriving.astype(jnp.int32).reshape(shaped), axis=2) - 1
    device_base = lax.broadcasted_iota(jnp.int32, in_order.shape, 1) * slot_count
    wanted = (device_base + in_order).reshape(layer_count, group_size * capacity)
    anchor = jnp.take_along_axis(source, wanted, axis=1)
    sender = anchor // slot_count
    list_place = jnp.clip(jnp.take_along_axis(out_rank, anchor, axis=1), 0, capacity - 1)
    gather_index = (list_place * group_size + sender).reshape(layer_count, group_size, capacity)
    gather_index = jnp.transpose(gather_index, (0, 2, 1)).reshape(
        layer_count, capacity * group_size
    )
    my_out = lax.dynamic_index_in_dim(out_order, my_index, axis=1, keepdims=False)
    my_arrive = lax.dynamic_index_in_dim(arriving.reshape(shaped), my_index, axis=1, keepdims=False)
    my_rank = jnp.clip(
        lax.dynamic_index_in_dim(in_rank, my_index, axis=1, keepdims=False), 0, capacity - 1
    )
    return (capacity, my_out, gather_index, my_arrive, my_rank)


def relocate(arrays, route_plan, group_size):
    capacity, my_out, gather_index, my_arrive, my_rank = route_plan
    layer_count, slot_count, row_count, col_count = arrays[0].shape
    flat_size = row_count * col_count
    piece_size = flat_size // group_size
    packed = tuple(
        (
            pick_rows(member.reshape(layer_count, slot_count, flat_size), my_out).reshape(
                layer_count, capacity, group_size, piece_size
            )
            for member in arrays
        )
    )
    spread = lax.all_to_all(packed, EXPERT, split_axis=2, concat_axis=2, tiled=True)
    regrouped = tuple(
        (
            pick_rows(
                member.reshape(layer_count, capacity * group_size, piece_size), gather_index
            ).reshape(layer_count, capacity, group_size, piece_size)
            for member in spread
        )
    )
    landed = lax.all_to_all(regrouped, EXPERT, split_axis=2, concat_axis=2, tiled=True)
    results = []
    for member, initial in zip(landed, arrays):
        arrived = pick_rows(member.reshape(layer_count, capacity, flat_size), my_rank).reshape(
            initial.shape
        )
        results.append(jnp.where(my_arrive[:, :, None, None], arrived, initial))
    return tuple(results)


def shards(master, moment_one, moment_two, gradient, old_slot, new_slot):
    layer_count, slot_count, row_count, col_count = master.shape
    group_size = lax.axis_size(EXPERT)
    entry_count = (
        layer_count * slot_count * group_size * row_count * lax.axis_size("dp") * col_count
    )
    my_index = lax.axis_index(EXPERT)
    route_plan = build_plan(old_slot, new_slot, slot_count, group_size, my_index)
    clip_scale = clip_factor(grad_total(gradient), entry_count)
    updated = adam_update(master, moment_one, moment_two, gradient, clip_scale)
    return relocate(updated, route_plan, group_size)


def solution(mesh):
    split = Mesh(
        mesh.devices.reshape(mesh.shape["dp"], 4, 4, 2), ("dp", "expert_0", "expert_1", "expert_2")
    )
    return jax.shard_map(
        shards,
        mesh=split,
        in_specs=(
            P(None, EXPERT, "dp", None),
            P(None, EXPERT, "dp", None),
            P(None, EXPERT, "dp", None),
            P(None, EXPERT, "dp", None),
            P(),
            P(),
        ),
        out_specs=(
            P(None, EXPERT, "dp", None),
            P(None, EXPERT, "dp", None),
            P(None, EXPERT, "dp", None),
        ),
        check_vma=False,
    )
```

profile of v0, /device:TPU:1, one launch (start us, length us, event | category | flops | bytes accessed | tf_op | source)
XLA Modules:
  0.0 211.4 jit_solution(510787888147914341)
XLA Ops:
  10.7 9.9 %psum.28 = f32[]{:T(128)} all-reduce(f32[]{:T(128)} %fusion.2), channel_id=1, replica_groups=mesh['dp'=4,'expert_0'=4,'expert_1'=4,'expert_2'=2] {'dp'}, use_global_device_ids=true, to_apply=%region_2.4 | all-reduce | flops 1 | bytes 8 | tf_op jit(solution)/shard_map/psum | solution.py:26
  20.6 10.4 %psum.29 = f32[]{:T(128)} all-reduce(f32[]{:T(128)} %psum.28), channel_id=1, replica_groups=mesh['dp'=4,'expert_0'=4,'expert_1'=4,'expert_2'=2] {'expert_0'}, use_global_device_ids=true, to_apply=%region_3.5 | all-reduce | flops 1 | bytes 8 | tf_op jit(solution)/shard_map/psum | solution.py:26
  31.0 9.3 %psum.30 = f32[]{:T(128)} all-reduce(f32[]{:T(128)} %psum.29), channel_id=1, replica_groups=mesh['dp'=4,'expert_0'=4,'expert_1'=4,'expert_2'=2] {'expert_1'}, use_global_device_ids=true, to_apply=%region_4.6 | all-reduce | flops 1 | bytes 8 | tf_op jit(solution)/shard_map/psum | solution.py:26
  40.3 9.5 %psum.31 = f32[]{:T(128)} all-reduce(f32[]{:T(128)} %psum.30), channel_id=1, replica_groups=mesh['dp'=4,'expert_0'=4,'expert_1'=4,'expert_2'=2] {'expert_2'}, use_global_device_ids=true, to_apply=%region_5.7 | all-reduce | flops 1 | bytes 8 | tf_op jit(solution)/shard_map/psum | solution.py:26
  50.5 4.9 %multiply_subtract_fusion = (f32[2,4,16,2880]{3,2,1,0:T(8,128)S(1)}, f32[2,4,16,2880]{3,2,1,0:T(8,128)S(1)}, f32[2,4,16,2880]{3,2,1,0:T(8,128)}) fusion(f32[2,4,16,2880]{3,2,1,0:T(8,128)} %param.16, f32[]{:T(128)S(6)} %min_shard_map.3, bf16[2,4,16,2880]{3,2,1,0:T(8,128)(2,1)} %param.19, f32[2,4,16,2880]{3,2,1,0:T(8,128)} %param.17, f32[2,4,16,2880]{3,2,1,0:T(8,128)} %param.18), kind=kLoop, calls=%fused_computation.20 | loop fusion | flops 6266880 | bytes 9584644 | tf_op jit(solution)/shard_map/sub | solution.py:34
  59.4 3.2 %reshape.178 = f32[2,4,46080]{2,1,0:T(4,128)} reshape(f32[2,4,16,2880]{3,2,1,0:T(8,128)} %get-tuple-element.25) | data formatting | bytes 2949120 | tf_op jit(solution)/shard_map/reshape | solution.py:98
  63.3 2.4 %gather_fusion.1 = s32[256]{0:T(256)S(1)} fusion(s32[2,128]{1,0:T(2,128)S(1)} %copy-done, s32[256]{0:T(256)S(1)} %get-tuple-element.38), kind=kCustom, calls=%fused_computation.5.clone | custom fusion | bytes 4096 | tf_op jit(solution)/shard_map/jit(take_along_axis)/gather | solution.py:58
  67.4 2.4 %gather_fusion = s32[256]{0:T(256)S(1)} fusion(s32[2,128]{1,0:T(2,128)S(1)} %copy-done.1, s32[256]{0:T(256)S(1)} %get-tuple-element.39), kind=kCustom, calls=%fused_computation.clone | custom fusion | bytes 4096 | tf_op jit(solution)/shard_map/jit(take_along_axis)/gather | solution.py:57
  70.1 2.8 %gather_fusion.2 = f32[2,46080]{1,0:T(2,128)S(1)} fusion(f32[2,4,46080]{2,1,0:T(4,128)} %reshape.160, s32[2]{0:T(128)S(1)} %or_bitcast_fusion), kind=kCustom, calls=%fused_computation.1.clone | custom fusion | bytes 737296 | tf_op jit(solution)/shard_map/vmap(jit(_take))/gather | solution.py:48
  72.9 2.7 %gather_fusion.7 = f32[2,46080]{1,0:T(2,128)} fusion(f32[2,4,46080]{2,1,0:T(4,128)S(1)} %copy-done.4, s32[2]{0:T(128)S(1)} %or_bitcast_fusion), kind=kCustom, calls=%fused_computation.6.clone | custom fusion | bytes 737296 | tf_op jit(solution)/shard_map/vmap(jit(_take))/gather | solution.py:48
  75.6 2.7 %gather_fusion.10 = f32[2,46080]{1,0:T(2,128)S(1)} fusion(f32[2,4,46080]{2,1,0:T(4,128)} %reshape.178, s32[2]{0:T(128)S(1)} %or_bitcast_fusion), kind=kCustom, calls=%fused_computation.7.clone | custom fusion | bytes 737296 | tf_op jit(solution)/shard_map/vmap(jit(_take))/gather | solution.py:48
  82.2 3.9 %all-to-all-start.4 = ((f32[2,1,32,1440]{3,0,1,2:T(2,128)}), f32[2,1,32,1440]{3,0,1,2:T(2,128)S(1)}, u32[]{:S(2)}, u32[]{:S(2)}) async-start(f32[2,1,32,1440]{3,0,1,2:T(2,128)} %copy.62), calls=%async_computation.4 | async-start | bytes 786432 | tf_op jit(solution)/shard_map/all_to_all | solution.py:104
  89.3 7.0 %all-to-all-done.4 = f32[2,1,32,1440]{3,0,1,2:T(2,128)S(1)} async-done(((f32[2,1,32,1440]{3,0,1,2:T(2,128)}), f32[2,1,32,1440]{3,0,1,2:T(2,128)S(1)}, u32[]{:S(2)}, u32[]{:S(2)}) %all-to-all-start.4) | async-done | bytes 368672 | tf_op jit(solution)/shard_map/all_to_all | solution.py:104
  96.4 3.9 %all-to-all-start.2 = ((f32[2,1,32,1440]{3,0,1,2:T(2,128)}), f32[2,1,32,1440]{3,0,1,2:T(2,128)S(1)}, u32[]{:S(2)}, u32[]{:S(2)}) async-start(f32[2,1,32,1440]{3,0,1,2:T(2,128)} %copy.54), calls=%async_computation.2 | async-start | bytes 786432 | tf_op jit(solution)/shard_map/all_to_all | solution.py:104
  103.3 7.1 %all-to-all-done.2 = f32[2,1,32,1440]{3,0,1,2:T(2,128)S(1)} async-done(((f32[2,1,32,1440]{3,0,1,2:T(2,128)}), f32[2,1,32,1440]{3,0,1,2:T(2,128)S(1)}, u32[]{:S(2)}, u32[]{:S(2)}) %all-to-all-start.2) | async-done | bytes 368672 | tf_op jit(solution)/shard_map/all_to_all | solution.py:104
  110.4 3.8 %all-to-all-start = ((f32[2,1,32,1440]{3,0,1,2:T(2,128)}), f32[2,1,32,1440]{3,0,1,2:T(2,128)S(1)}, u32[]{:S(2)}, u32[]{:S(2)}) async-start(f32[2,1,32,1440]{3,0,1,2:T(2,128)} %copy.46), calls=%async_computation | async-start | bytes 786432 | tf_op jit(solution)/shard_map/all_to_all | solution.py:104
  116.9 7.6 %all-to-all-done = f32[2,1,32,1440]{3,0,1,2:T(2,128)S(1)} async-done(((f32[2,1,32,1440]{3,0,1,2:T(2,128)}), f32[2,1,32,1440]{3,0,1,2:T(2,128)S(1)}, u32[]{:S(2)}, u32[]{:S(2)}) %all-to-all-start) | async-done | bytes 368672 | tf_op jit(solution)/shard_map/all_to_all | solution.py:104
  127.7 13.6 %all_to_all.30 = f32[2,1,32,1440]{3,0,1,2:T(2,128)S(1)} all-to-all(f32[2,1,32,1440]{3,0,1,2:T(2,128)S(1)} %get-tuple-element.26), channel_id=1, replica_groups=mesh['dp'=4,'expert_0'=4,'expert_1'=4,'expert_2'=2] {'expert_0','expert_..., dimensions={2} | all-to-all | bytes 737280 | tf_op jit(solution)/shard_map/all_to_all | solution.py:113
  141.4 3.8 %all-to-all-start.3 = ((f32[2,1,32,1440]{3,0,1,2:T(2,128)}), f32[2,1,32,1440]{3,0,1,2:T(2,128)S(1)}, u32[]{:S(2)}, u32[]{:S(2)}) async-start(f32[2,1,32,1440]{3,0,1,2:T(2,128)} %get-tuple-element.27), calls=%async_computation.3 | async-start | bytes 786432 | tf_op jit(solution)/shard_map/all_to_all | solution.py:113
  145.7 9.7 %all-to-all-done.3 = f32[2,1,32,1440]{3,0,1,2:T(2,128)S(1)} async-done(((f32[2,1,32,1440]{3,0,1,2:T(2,128)}), f32[2,1,32,1440]{3,0,1,2:T(2,128)S(1)}, u32[]{:S(2)}, u32[]{:S(2)}) %all-to-all-start.3) | async-done | bytes 368672 | tf_op jit(solution)/shard_map/all_to_all | solution.py:113
  155.5 3.9 %all-to-all-start.1 = ((f32[2,1,32,1440]{3,0,1,2:T(2,128)}), f32[2,1,32,1440]{3,0,1,2:T(2,128)S(1)}, u32[]{:S(2)}, u32[]{:S(2)}) async-start(f32[2,1,32,1440]{3,0,1,2:T(2,128)} %get-tuple-element.28), calls=%async_computation.1 | async-start | bytes 786432 | tf_op jit(solution)/shard_map/all_to_all | solution.py:113
  160.8 8.8 %all-to-all-done.1 = f32[2,1,32,1440]{3,0,1,2:T(2,128)S(1)} async-done(((f32[2,1,32,1440]{3,0,1,2:T(2,128)}), f32[2,1,32,1440]{3,0,1,2:T(2,128)S(1)}, u32[]{:S(2)}, u32[]{:S(2)}) %all-to-all-start.1) | async-done | bytes 368672 | tf_op jit(solution)/shard_map/all_to_all | solution.py:113
  170.2 2.8 %gather_fusion.6 = f32[8,46080]{1,0:T(8,128)} fusion(f32[2,1,46080]{2,1,0:T(1,128)S(1)} %reshape.169, s32[8]{0:T(128)S(1)} %reshape.353), kind=kCustom, calls=%fused_computation.4.clone | custom fusion | bytes 2949184 | tf_op jit(solution)/shard_map/vmap(jit(_take))/gather | solution.py:48
  172.9 2.9 %reshape.356 = f32[2,4,46080]{2,1,0:T(4,128)} reshape(f32[8,46080]{1,0:T(8,128)} %gather_fusion.6) | data formatting | bytes 2949120 | tf_op jit(solution)/shard_map/vmap(jit(_take))/gather | solution.py:48
  175.9 2.8 %gather_fusion.9 = f32[8,46080]{1,0:T(8,128)} fusion(f32[2,1,46080]{2,1,0:T(1,128)S(1)} %reshape.176, s32[8]{0:T(128)S(1)} %reshape.353), kind=kCustom, calls=%fused_computation.11.clone | custom fusion | bytes 2949184 | tf_op jit(solution)/shard_map/vmap(jit(_take))/gather | solution.py:48
  178.6 2.9 %reshape.371 = f32[2,4,46080]{2,1,0:T(4,128)} reshape(f32[8,46080]{1,0:T(8,128)} %gather_fusion.9) | data formatting | bytes 2949120 | tf_op jit(solution)/shard_map/vmap(jit(_take))/gather | solution.py:48
  181.6 2.8 %gather_fusion.12 = f32[8,46080]{1,0:T(8,128)} fusion(f32[2,1,46080]{2,1,0:T(1,128)S(1)} %reshape.182, s32[8]{0:T(128)S(1)} %reshape.353), kind=kCustom, calls=%fused_computation.12.clone | custom fusion | bytes 2949184 | tf_op jit(solution)/shard_map/vmap(jit(_take))/gather | solution.py:48
  184.3 3.0 %reshape.386 = f32[2,4,46080]{2,1,0:T(4,128)} reshape(f32[8,46080]{1,0:T(8,128)} %gather_fusion.12) | data formatting | bytes 2949120 | tf_op jit(solution)/shard_map/vmap(jit(_take))/gather | solution.py:48
  187.3 4.5 %broadcast_select_fusion.3 = (f32[2,4,46080]{2,1,0:T(4,128)}, f32[2,4,46080]{2,1,0:T(4,128)}, f32[2,4,46080]{2,1,0:T(4,128)}) fusion(f32[2,4,46080]{2,1,0:T(4,128)} %reshape.386, pred[2,4]{1,0:T(4,128)(4,1)S(1)} %compare_and_fusion, f32[2,4,46080]{2,1,0:T(4,128)} %reshape.371, f32[2,4,46080]{2,1,0:T(4,128)S(1)} %copy-done.5), kind=kLoop, calls=%fused_computation.24 | loop fusion | flops 1105920 | bytes 8847368 | tf_op jit(solution)/shard_map/vmap(jit(_take))/select_n | solution.py:48
  191.8 2.9 %reshape.183 = f32[2,4,16,2880]{3,2,1,0:T(8,128)} reshape(f32[2,4,46080]{2,1,0:T(4,128)} %get-tuple-element.32) | data formatting | bytes 2949120 | tf_op jit(solution)/shard_map/reshape | solution.py:116
  196.5 2.9 %reshape.171 = f32[2,4,16,2880]{3,2,1,0:T(8,128)} reshape(f32[2,4,46080]{2,1,0:T(4,128)} %get-tuple-element.34) | data formatting | bytes 2949120 | tf_op jit(solution)/shard_map/reshape | solution.py:116
  199.5 5.1 %broadcast_select_fusion = (f32[2,4,16,2880]{3,2,1,0:T(8,128)}, f32[2,4,16,2880]{3,2,1,0:T(8,128)}, f32[2,4,16,2880]{3,2,1,0:T(8,128)}) fusion(f32[2,4,16,2880]{3,2,1,0:T(8,128)} %reshape.183, f32[2,4,16,2880]{3,2,1,0:T(8,128)} %get-tuple-element.25, pred[2,4]{1,0:T(4,128)(4,1)S(1)} %bitcast.112, f32[2,4,16,2880]{3,2,1,0:T(8,128)} %reshape.177, ...), kind=kLoop, calls=%fused_computation.21 | loop fusion | flops 1105920 | bytes 13271048 | tf_op jit(solution)/shard_map/jit(_where)/select_n | solution.py:119
  (98 shorter events, 30.3 us)
Async XLA Ops:
  7.2 55.4 %sort.65.cloned.1.call-start = ((), (), s32[]{:S(2)}) async-start(), calls=%async_computation.7 | async-start | bytes 6176 | tf_op jit(solution)/shard_map/jit(argsort)/sort | solution.py:56
  7.9 54.7 %sort.63.cloned.1.call-start = ((), (), s32[]{:S(2)}) async-start(), calls=%async_computation.6 | async-start | bytes 6176 | tf_op jit(solution)/shard_map/jit(argsort)/sort | solution.py:55
  55.4 2.0 copy-start.2
  59.4 3.9 %copy-start = (s32[2,128]{1,0:T(2,128)S(1)}, s32[2,128]{1,0:T(2,128)}, u32[]{:S(2)}) copy-start(s32[2,128]{1,0:T(2,128)} %param.21) | copy-start | bytes 3076
  59.4 8.0 %copy-start.1 = (s32[2,128]{1,0:T(2,128)S(1)}, s32[2,128]{1,0:T(2,128)}, u32[]{:S(2)}) copy-start(s32[2,128]{1,0:T(2,128)} %param.20) | copy-start | bytes 3076
  62.6 7.2 %copy-start.9 = (s32[2,128]{1,0:T(2,128)S(1)}, s32[2,128]{1,0:T(2,128)}, u32[]{:S(2)}) copy-start(s32[2,128]{1,0:T(2,128)} %get-tuple-element.12) | copy-start | bytes 3076
  70.1 2.8 %copy-start.4 = (f32[2,4,46080]{2,1,0:T(4,128)S(1)}, f32[2,4,46080]{2,1,0:T(4,128)}, u32[]{:S(2)}) copy-start(f32[2,4,46080]{2,1,0:T(4,128)} %reshape.172) | copy-start | bytes 4423684
  75.6 2.7 %copy-start.7 = (f32[2,46080]{1,0:T(2,128)S(1)}, f32[2,46080]{1,0:T(2,128)}, u32[]{:S(2)}) copy-start(f32[2,46080]{1,0:T(2,128)} %gather_fusion.7) | copy-start | bytes 1105924
  82.2 14.2 %all-to-all-start.4 = ((f32[2,1,32,1440]{3,0,1,2:T(2,128)}), f32[2,1,32,1440]{3,0,1,2:T(2,128)S(1)}, u32[]{:S(2)}, u32[]{:S(2)}) async-start(f32[2,1,32,1440]{3,0,1,2:T(2,128)} %copy.62), calls=%async_computation.4 | async-start | bytes 786432 | tf_op jit(solution)/shard_map/all_to_all | solution.py:104
  88.3 13.6 %copy-start.8 = (f32[2,1,46080]{2,0,1:T(2,128)S(1)}, f32[2,1,46080]{2,0,1:T(2,128)}, u32[]{:S(2)}) copy-start(f32[2,1,46080]{2,0,1:T(2,128)} %get-tuple-element.37) | copy-start | bytes 1105924
  96.4 14.1 %all-to-all-start.2 = ((f32[2,1,32,1440]{3,0,1,2:T(2,128)}), f32[2,1,32,1440]{3,0,1,2:T(2,128)S(1)}, u32[]{:S(2)}, u32[]{:S(2)}) async-start(f32[2,1,32,1440]{3,0,1,2:T(2,128)} %copy.54), calls=%async_computation.2 | async-start | bytes 786432 | tf_op jit(solution)/shard_map/all_to_all | solution.py:104
  110.4 14.1 %all-to-all-start = ((f32[2,1,32,1440]{3,0,1,2:T(2,128)}), f32[2,1,32,1440]{3,0,1,2:T(2,128)S(1)}, u32[]{:S(2)}, u32[]{:S(2)}) async-start(f32[2,1,32,1440]{3,0,1,2:T(2,128)} %copy.46), calls=%async_computation | async-start | bytes 786432 | tf_op jit(solution)/shard_map/all_to_all | solution.py:104
  141.4 14.1 %all-to-all-start.3 = ((f32[2,1,32,1440]{3,0,1,2:T(2,128)}), f32[2,1,32,1440]{3,0,1,2:T(2,128)S(1)}, u32[]{:S(2)}, u32[]{:S(2)}) async-start(f32[2,1,32,1440]{3,0,1,2:T(2,128)} %get-tuple-element.27), calls=%async_computation.3 | async-start | bytes 786432 | tf_op jit(solution)/shard_map/all_to_all | solution.py:113
  155.5 14.1 %all-to-all-start.1 = ((f32[2,1,32,1440]{3,0,1,2:T(2,128)}), f32[2,1,32,1440]{3,0,1,2:T(2,128)S(1)}, u32[]{:S(2)}, u32[]{:S(2)}) async-start(f32[2,1,32,1440]{3,0,1,2:T(2,128)} %get-tuple-element.28), calls=%async_computation.1 | async-start | bytes 786432 | tf_op jit(solution)/shard_map/all_to_all | solution.py:113
  184.3 3.0 %copy-start.5 = (f32[2,4,46080]{2,1,0:T(4,128)S(1)}, f32[2,4,46080]{2,1,0:T(4,128)}, u32[]{:S(2)}) copy-start(f32[2,4,46080]{2,1,0:T(4,128)} %reshape.356) | copy-start | bytes 4423684
  191.8 3.0 %copy-start.6 = (f32[2,4,46080]{2,1,0:T(4,128)S(1)}, f32[2,4,46080]{2,1,0:T(4,128)}, u32[]{:S(2)}) copy-start(f32[2,4,46080]{2,1,0:T(4,128)} %get-tuple-element.33) | copy-start | bytes 4423684
  196.5 2.9 %copy-start.3 = (f32[2,4,16,2880]{3,2,1,0:T(8,128)S(1)}, f32[2,4,16,2880]{3,2,1,0:T(8,128)}, u32[]{:S(2)}) copy-start(f32[2,4,16,2880]{3,2,1,0:T(8,128)} %copy-done.2) | copy-start | bytes 4423684
Sparse Core Ops, SparseCore 0:
  10.2 2.2 sort.69.cloned.1.call-done
  15.0 2.2 sort.67.cloned.1.call-done
  (2 shorter events, 0.0 us)
where the time goes:
time: 212 us; the launch traced here: 211 us
  local copies, waits for them, and re-layouts  60.5 us (29%)
  blocking collectives  52.7 us (25%)
  waiting for transfers between devices  40.3 us (19%)
  other arithmetic  23.5 us (11%)
  starting transfers between devices  19.3 us (9%)
  between operations  15.1 us (7%)
    psum x4, blocking collectives, by_axis(): return functools.reduce(lax.psum, axes, value)  39.1 us
    gather x14, local copies, waits for them, and re-layouts, pick_rows(): jnp.take(layer_block, layer_pick, axis=0)  28.8 us
    all_to_all x3, waiting for transfers between devices, relocate(): lax.all_to_all(packed, EXPERT, split_axis=2, concat_axis=2, tiled=True)  21.8 us
    all_to_all x2, waiting for transfers between devices, relocate(): lax.all_to_all(regrouped, EXPERT, split_axis=2, concat_axis=2, tiled=True)  18.5 us
    all_to_all x1, blocking collectives, relocate(): lax.all_to_all(regrouped, EXPERT, split_axis=2, concat_axis=2, tiled=True)  13.6 us
    all_to_all x3, starting transfers between devices, relocate(): lax.all_to_all(packed, EXPERT, split_axis=2, concat_axis=2, tiled=True)  11.6 us
    all_to_all x2, starting transfers between devices, relocate(): lax.all_to_all(regrouped, EXPERT, split_axis=2, concat_axis=2, tiled=True)  7.7 us
    reshape x3, local copies, waits for them, and re-layouts, relocate(): pick_rows(member.reshape(layer_count, capacity, flat_size), my_rank)  7.61 us
  transfers between devices with their start and end apart: 5, of which 5 were waited for; matrix products, arithmetic and copies ran while one was open for 5% of the time, Pallas kernels for 0%

commit v1 on v0

v1 whole, which is shorter than its diff:
```python
import functools
import math

import jax
import jax.numpy as jnp
from jax import lax
from jax.experimental import pallas as pl
from jax.experimental.pallas import tpu as pltpu
from jax.sharding import PartitionSpec as P

BETA_ONE = 0.9
BETA_TWO = 0.95
LEARN_RATE = 0.05
DECAY_RATE = 0.1
ADAM_EPS = 1e-08
CLIP_RMS = 2.0
FIRST_FIX = 1.0 - 0.9**10
SECOND_FIX = 1.0 - 0.95**10

ZDIM, YDIM, CORES = 4, 4, 2
GROUP = ZDIM * YDIM * CORES
DP = 4
LANES = 128
SUB = 4
PIECE = 3
HOLDERS = 30


def move_order():
    moves = [
        (dz, dy, dc)
        for dz in (0, 1, 2, -1)
        for dy in (0, 1, 2, -1)
        for dc in (0, 1)
        if (dz, dy, dc) != (0, 0, 0)
    ]
    neg = lambda v: v if v == 2 else -v
    order = []
    for dz, dy, dc in sorted(moves, key=lambda m: -(abs(m[0]) + abs(m[1]))):
        for m in ((dz, dy, dc), (neg(dz), neg(dy), dc), (dy, dz, dc), (neg(dy), neg(dz), dc)):
            if m not in order:
                order.append(m)
    return order


MOVES = move_order()


def shifted(me, move, sign=1):
    dz, dy, dc = move
    core, y, z = me % CORES, (me // CORES) % YDIM, me // (CORES * YDIM)
    z = (z + sign * dz + ZDIM) % ZDIM
    y = (y + sign * dy + YDIM) % YDIM
    return (z * YDIM + y) * CORES + (core + dc) % CORES


def adam(master, moment_one, moment_two, gradient, scale):
    scaled = gradient * scale
    first = BETA_ONE * moment_one + (1.0 - BETA_ONE) * scaled
    second = BETA_TWO * moment_two + (1.0 - BETA_TWO) * scaled * scaled
    step = (first * (1.0 / FIRST_FIX)) / (jnp.sqrt(second * (1.0 / SECOND_FIX)) + ADAM_EPS)
    return master - LEARN_RATE * (step + DECAY_RATE * master), first, second


def exchange_kernel(
    entry_count,
    plan,
    master_hbm,
    one_hbm,
    two_hbm,
    grad_hbm,
    new_w,
    new_one,
    new_two,
    landed,
    master,
    one,
    two,
    grad,
    send_raw,
    send_new,
    hold_raw,
    hold_new,
    back_0,
    back_1,
    home,
    part,
    parts,
    line,
    lines,
    load_sem,
    part_send,
    part_recv,
    line_send,
    line_recv,
    out_send,
    out_recv,
    back_send,
    back_recv,
):
    layers, slots, rows, cols = master.shape
    full = cols // LANES
    dp = lax.axis_index("dp")
    me = lax.axis_index("expert")
    targets = [shifted(me, m) for m in MOVES]
    sources = [shifted(me, m, -1) for m in MOVES]

    loads = [
        pltpu.make_async_copy(src, dst, load_sem.at[i])
        for i, (src, dst) in enumerate(
            ((grad_hbm, grad), (master_hbm, master), (one_hbm, one), (two_hbm, two))
        )
    ]
    for load in loads:
        load.start()

    barrier = pltpu.get_barrier_semaphore()
    for t in targets:
        pl.semaphore_signal(barrier, inc=1, device_id={"expert": t})
    for d in range(1, DP):
        pl.semaphore_signal(barrier, inc=1, device_id={"dp": (dp + d) % DP})

    loads[0].wait()

    def square(i, acc):
        for c in range(full):
            g = grad[i // slots, i % slots, :, c * LANES : (c + 1) * LANES].astype(jnp.float32)
            acc = acc + g * g
        return acc

    acc = lax.fori_loop(
        0, layers * slots, square, jnp.zeros((rows, LANES), jnp.float32)
    )
    tail = grad[:, :, :, full * LANES :].astype(jnp.float32)
    tail = jnp.sum((tail * tail).reshape(layers * slots * rows, cols - full * LANES), axis=0, keepdims=True)
    acc = jnp.sum(acc, axis=0, keepdims=True)
    part[...] = acc + jnp.concatenate([tail, jnp.zeros_like(tail)], axis=1)
    parts[pl.ds(me, 1)] = part[...].reshape(1, 1, LANES)

    for load in loads[1:]:
        load.wait()

    my_move = [plan[layer, me] % slots for layer in range(layers)]

    def units(x):
        return x.reshape(rows // SUB, SUB, LANES)

    def joined(x):
        x = x.reshape(rows // SUB // 2, 2, SUB, cols - full * LANES)
        return jnp.concatenate([x[:, 0], x[:, 1]], axis=-1)

    for i, ref in enumerate((master, one, two, grad)):
        for c in range(full):
            x = ref[0, my_move[0], :, c * LANES : (c + 1) * LANES].astype(jnp.float32)
            send_raw[4 * c : 4 * c + 4, i] = units(x)
        x = ref[0, my_move[0], :, full * LANES :].astype(jnp.float32)
        send_raw[4 * full : 4 * full + 2, i] = joined(x)

    pl.semaphore_wait(barrier, len(MOVES) + DP - 1)

    part_copies = []
    for k, t in enumerate(targets):
        copy = pltpu.make_async_remote_copy(
            part, parts.at[me], part_send.at[k], part_recv.at[k], device_id={"expert": t}
        )
        copy.start()
        part_copies.append(copy)

    def out(send, hold, layer, start):
        for k, t in enumerate(targets):
            copy = pltpu.make_async_remote_copy(
                send.at[pl.ds(PIECE * t, PIECE)],
                hold.at[me],
                out_send.at[layer, k],
                out_recv.at[layer, k],
                device_id={"expert": t},
            )
            if start:

                @pl.when(t < HOLDERS)
                def _():
                    copy.start()
            else:

                @pl.when(t < HOLDERS)
                def _():
                    copy.wait_send()

    def arrived(send, hold, layer):
        @pl.when(me < HOLDERS)
        def _():
            for k, t in enumerate(targets):
                pltpu.make_async_remote_copy(
                    send.at[pl.ds(0, PIECE)],
                    hold.at[me],
                    out_send.at[layer, k],
                    out_recv.at[layer, k],
                    device_id={"expert": t},
                ).wait_recv()

    def back(buf, layer, start):
        @pl.when(me < HOLDERS)
        def _():
            for k, t in enumerate(targets):
                copy = pltpu.make_async_remote_copy(
                    buf.at[t],
                    home.at[layer, pl.ds(PIECE * me, PIECE)],
                    back_send.at[layer, k],
                    back_recv.at[layer, k],
                    device_id={"expert": t},
                )
                if start:
                    copy.start()
                else:
                    copy.wait_send()

    def returned(buf, layer):
        for k, s in enumerate(sources):

            @pl.when(s < HOLDERS)
            def _():
                pltpu.make_async_remote_copy(
                    buf.at[0],
                    home.at[layer, pl.ds(0, PIECE)],
                    back_send.at[layer, k],
                    back_recv.at[layer, k],
                    device_id={"expert": s},
                ).wait_recv()

    out(send_raw, hold_raw, 0, True)
    hold_raw[pl.ds(me, 1)] = send_raw[pl.ds(PIECE * me, PIECE)][None]

    for copy in part_copies:
        copy.wait_recv()
    plane = jnp.sum(parts[...].reshape(GROUP, LANES), axis=0, keepdims=True)
    line[...] = plane
    lines[pl.ds(dp, 1)] = plane.reshape(1, 1, LANES)
    line_copies = []
    for d in range(1, DP):
        copy = pltpu.make_async_remote_copy(
            line,
            lines.at[dp],
            line_send.at[d - 1],
            line_recv.at[d - 1],
            device_id={"dp": (dp + d) % DP},
        )
        copy.start()
        line_copies.append(copy)
    for copy in line_copies:
        copy.wait_recv()
    total = jnp.sum(lines[...].reshape(DP, LANES), axis=0, keepdims=True)
    total = jnp.sum(total, axis=1, keepdims=True)
    scale = jnp.minimum(1.0, CLIP_RMS * math.sqrt(entry_count) / (jnp.sqrt(total) + 1e-06))

    for c in range(full):
        at = (1, my_move[1], slice(None), slice(c * LANES, (c + 1) * LANES))
        done = adam(master[at], one[at], two[at], grad[at].astype(jnp.float32), scale)
        for i, x in enumerate(done):
            send_new[4 * c : 4 * c + 4, i] = units(x)
    at = (1, my_move[1], slice(None), slice(full * LANES, cols))
    done = adam(master[at], one[at], two[at], grad[at].astype(jnp.float32), scale)
    for i, x in enumerate(done):
        send_new[4 * full : 4 * full + 2, i] = joined(x)
    out(send_new, hold_new, 1, True)
    hold_new[pl.ds(me, 1)] = send_new[pl.ds(PIECE * me, PIECE)][None]

    def resident(i, _):
        layer, slot = i // slots, i % slots
        for lo in range(0, cols, 2 * LANES):
            at = (layer, slot, slice(None), slice(lo, min(lo + 2 * LANES, cols)))
            done = adam(master[at], one[at], two[at], grad[at].astype(jnp.float32), scale)
            for ref, x in zip((new_w, new_one, new_two), done):
                ref[at] = x
        return 0

    lax.fori_loop(0, layers * slots, resident, 0)

    arrived(send_raw, hold_raw, 0)

    def forward_raw(t, _):
        x = hold_raw[plan[0, t] // slots]
        done = adam(x[:, 0], x[:, 1], x[:, 2], x[:, 3], scale)
        for i, y in enumerate(done):
            back_0[t, :, i] = y
        return 0

    lax.fori_loop(0, GROUP, forward_raw, 0)
    back(back_0, 0, True)

    @pl.when(me < HOLDERS)
    def _():
        home[0, pl.ds(PIECE * me, PIECE)] = back_0[me]

    arrived(send_new, hold_new, 1)

    def forward_new(t, _):
        back_1[t] = hold_new[plan[1, t] // slots]
        return 0

    lax.fori_loop(0, GROUP, forward_new, 0)
    back(back_1, 1, True)

    @pl.when(me < HOLDERS)
    def _():
        home[1, pl.ds(PIECE * me, PIECE)] = back_1[me]

    def unpack(layer):
        for i in range(3):
            for c in range(full):
                x = home[layer, 4 * c : 4 * c + 4, i]
                landed[i, layer, :, c * LANES : (c + 1) * LANES] = x.reshape(rows, LANES)
            x = home[layer, 4 * full : 4 * full + 2, i]
            width = cols - full * LANES
            x = jnp.stack([x[:, :, :width], x[:, :, width:]], axis=1)
            landed[i, layer, :, full * LANES :] = x.reshape(rows, width)

    returned(back_0, 0)
    unpack(0)
    returned(back_1, 1)
    unpack(1)

    for copy in part_copies:
        copy.wait_send()
    for copy in line_copies:
        copy.wait_send()
    out(send_raw, hold_raw, 0, False)
    out(send_new, hold_new, 1, False)
    back(back_0, 0, False)
    back(back_1, 1, False)


def exchange(plan, master, moment_one, moment_two, gradient, entry_count):
    layers, slots, rows, cols = master.shape
    vmem = pl.BlockSpec(memory_space=pltpu.VMEM)
    f32 = jnp.float32
    units = PIECE * GROUP
    dma = pltpu.SemaphoreType.DMA
    peers = len(MOVES)
    return pl.pallas_call(
        functools.partial(exchange_kernel, entry_count),
        out_shape=[jax.ShapeDtypeStruct(master.shape, f32)] * 3
        + [jax.ShapeDtypeStruct((3, layers, rows, cols), f32)],
        in_specs=[pl.BlockSpec(memory_space=pltpu.SMEM)] + [pl.BlockSpec(memory_space=pl.ANY)] * 4,
        out_specs=[vmem] * 4,
        scratch_shapes=[
            pltpu.VMEM(master.shape, f32),
            pltpu.VMEM(master.shape, f32),
            pltpu.VMEM(master.shape, f32),
            pltpu.VMEM(master.shape, jnp.bfloat16),
            pltpu.VMEM((units, 4, SUB, LANES), f32),
            pltpu.VMEM((units, 3, SUB, LANES), f32),
            pltpu.VMEM((GROUP, PIECE, 4, SUB, LANES), f32),
            pltpu.VMEM((GROUP, PIECE, 3, SUB, LANES), f32),
            pltpu.VMEM((GROUP, PIECE, 3, SUB, LANES), f32),
            pltpu.VMEM((GROUP, PIECE, 3, SUB, LANES), f32),
            pltpu.VMEM((layers, units, 3, SUB, LANES), f32),
            pltpu.VMEM((1, LANES), f32),
            pltpu.VMEM((GROUP, 1, LANES), f32),
            pltpu.VMEM((1, LANES), f32),
            pltpu.VMEM((DP, 1, LANES), f32),
            dma((4,)),
            dma((peers,)),
            dma((peers,)),
            dma((DP - 1,)),
            dma((DP - 1,)),
            dma((layers, peers)),
            dma((layers, peers)),
            dma((layers, peers)),
            dma((layers, peers)),
        ],
        compiler_params=pltpu.CompilerParams(
            collective_id=0, has_side_effects=True, vmem_limit_bytes=40 * 1024 * 1024
        ),
        name="exchange",
    )(plan, master, moment_one, moment_two, gradient)


def place_kernel(plan, mine, w, one, two, landed, out_w, out_one, out_two, sem):
    layers, slots = w.shape[:2]
    for phase in (0, 1):
        for layer in range(layers):
            moved = plan[layer, mine[0]] % slots
            for i, (src, dst) in enumerate(((w, out_w), (one, out_one), (two, out_two))):
                for slot in range(slots):

                    @pl.when(slot != moved)
                    def _():
                        copy = pltpu.make_async_copy(
                            src.at[layer, slot], dst.at[layer, slot], sem.at[i, layer, slot]
                        )
                        copy.start() if phase == 0 else copy.wait()

                    @pl.when(slot == moved)
                    def _():
                        copy = pltpu.make_async_copy(
                            landed.at[i, layer], dst.at[layer, slot], sem.at[i, layer, slot]
                        )
                        copy.start() if phase == 0 else copy.wait()


def place(plan, mine, w, one, two, landed):
    layers, slots = w.shape[:2]
    vmem = pl.BlockSpec(memory_space=pltpu.VMEM)
    smem = pl.BlockSpec(memory_space=pltpu.SMEM)
    return pl.pallas_call(
        place_kernel,
        out_shape=[jax.ShapeDtypeStruct(w.shape, w.dtype)] * 3,
        in_specs=[smem, smem] + [vmem] * 4,
        out_specs=[pl.BlockSpec(memory_space=pl.ANY)] * 3,
        scratch_shapes=[pltpu.SemaphoreType.DMA((3, layers, slots))],
        name="place",
    )(plan, mine, w, one, two, landed)


def shards(master, moment_one, moment_two, gradient, old_slot, new_slot):
    layers, slots, rows, cols = master.shape
    entry_count = layers * slots * GROUP * rows * DP * cols
    moved = old_slot != new_slot
    word = (old_slot // slots) * slots + new_slot % slots
    here = (new_slot // slots)[:, None, :] == lax.broadcasted_iota(
        jnp.int32, (layers, GROUP, GROUP * slots), 1
    )
    plan = jnp.sum(jnp.where(here & moved[:, None, :], word[:, None, :], 0), axis=2)
    mine = lax.axis_index("expert").reshape(1)
    w, one, two, landed = exchange(plan, master, moment_one, moment_two, gradient, entry_count)
    return place(plan, mine, w, one, two, landed)


def solution(mesh):
    spec = P(None, "expert", "dp", None)
    return jax.shard_map(
        shards,
        mesh=mesh,
        in_specs=(spec, spec, spec, spec, P(), P()),
        out_specs=(spec, spec, spec),
        check_vma=False,
    )
```

time: 212 us -> 64 us (0.30)
  blocking collectives: 52.7 us -> 0 us
  Pallas kernels: 0 us -> 51.8 us
  local copies, waits for them, and re-layouts: 60.5 us -> 9.72 us
  waiting for transfers between devices: 40.3 us -> 0 us
  other arithmetic: 23.5 us -> 1.52 us
  starting transfers between devices: 19.3 us -> 0 us
  between operations: 15.1 us -> 0.67 us
    pallas_call x0 -> x2, Pallas kernels: none -> 51.8 us  [the longest x1 46.8 us: exchange(): pl.pallas_call(functools.partial(exchange_kernel, entry_count), out_shape...]
    all_to_all x5 -> x0, waiting for transfers between devices: 40.3 us -> none  [the longest x3 21.8 us: relocate(): lax.all_to_all(packed, EXPERT, split_axis=2, concat_axis=2, tiled=True)]
    psum x4 -> x0, blocking collectives: 39.1 us -> none  [by_axis(): return functools.reduce(lax.psum, axes, value)]
    gather x22 -> x0, local copies, waits for them, and re-layouts: 35.8 us -> none  [the longest x14 28.8 us: pick_rows(): jnp.take(layer_block, layer_pick, axis=0)]
    reshape x21 -> x0, local copies, waits for them, and re-layouts: 22.4 us -> none  [the longest x3 7.61 us: relocate(): pick_rows(member.reshape(layer_count, capacity, flat_size), my_rank)]
    all_to_all x5 -> x0, starting transfers between devices: 19.3 us -> none  [the longest x3 11.6 us: relocate(): lax.all_to_all(packed, EXPERT, split_axis=2, concat_axis=2, tiled=True)]
    all_to_all x1 -> x0, blocking collectives: 13.6 us -> none  [relocate(): lax.all_to_all(regrouped, EXPERT, split_axis=2, concat_axis=2, tiled=True)]
    select_n x5 -> x1, other arithmetic: 11 us -> 0.71 us  [shards(): new_slot // slots]
  transfers between devices with their start and end apart: 5 -> 0, of which waited for: 5 -> 0; matrix products, arithmetic and copies ran while one was open for 5% -> 0% of each run, Pallas kernels for 0% -> 0%
where the time goes in v1:
time: 64 us; the launch traced here: 63.7 us
  Pallas kernels  51.8 us (81%)
  local copies, waits for them, and re-layouts  9.72 us (15%)
  other arithmetic  1.52 us (2%)
  between operations  0.67 us (1%)
    pallas_call x1, Pallas kernels, exchange(): pl.pallas_call(functools.partial(exchange_kernel, entry_count), out_shape...  46.8 us
    unnamed x18, local copies, waits for them, and re-layouts  9.72 us
    pallas_call x1, Pallas kernels, place(): pl.pallas_call(place_kernel, out_shape=[jax.ShapeDtypeStruct(w.shape, w.d...  4.94 us

profile of v1, /device:TPU:1, one launch (start us, length us, event | category | flops | bytes accessed | tf_op | source)
XLA Modules:
  0.0 63.7 jit_solution(2900006844979013607)
XLA Ops:
  0.6 0.7 %ne.34 = pred[2,128]{1,0:T(4,128)(4,1)S(1)} compare(s32[2,128]{1,0:T(2,128)} %param.10, s32[2,128]{1,0:T(2,128)} %param.11), direction=NE | non-fusion elementwise | flops 256 | bytes 2304 | tf_op jit(solution)/shard_map/ne | solution.py:418
  1.3 0.7 %and_select_fusion.2 = (s32[2,128]{1,0:T(2,128)S(1)}, s32[2,128]{1,0:T(2,128)S(1)}) fusion(s32[2,128]{1,0:T(2,128)} %param.11, s32[2,128]{1,0:T(2,128)} %param.10), kind=kLoop, calls=%fused_computation.5 | loop fusion | flops 9216 | bytes 4096 | tf_op jit(solution)/shard_map/jit(floor_divide)/jit(_where)/select_n | solution.py:420
  2.0 0.1 select_reduce_fusion.plan
  2.2 0.0 copy-start
  2.2 1.4 %copy-done = f32[2,4,16,2880]{3,2,1,0:T(8,128)S(1)} copy-done((f32[2,4,16,2880]{3,2,1,0:T(8,128)S(1)}, f32[2,4,16,2880]{3,2,1,0:T(8,128)}, u32[]{:S(2)}) %copy-start) | copy-done | bytes 1474584
  3.6 0.0 copy-start.1
  3.6 1.4 %copy-done.1 = f32[2,4,16,2880]{3,2,1,0:T(8,128)S(1)} copy-done((f32[2,4,16,2880]{3,2,1,0:T(8,128)S(1)}, f32[2,4,16,2880]{3,2,1,0:T(8,128)}, u32[]{:S(2)}) %copy-start.1) | copy-done | bytes 1474584
  4.9 0.0 copy-start.2
  4.9 1.4 %copy-done.2 = f32[2,4,16,2880]{3,2,1,0:T(8,128)S(1)} copy-done((f32[2,4,16,2880]{3,2,1,0:T(8,128)S(1)}, f32[2,4,16,2880]{3,2,1,0:T(8,128)}, u32[]{:S(2)}) %copy-start.2) | copy-done | bytes 1474584
  6.3 0.0 copy-start.7
  6.3 1.1 %copy-done.7 = bf16[2,4,16,2880]{3,2,1,0:T(8,128)(2,1)S(1)} copy-done((bf16[2,4,16,2880]{3,2,1,0:T(8,128)(2,1)S(1)}, bf16[2,4,16,2880]{3,2,1,0:T(8,128)(2,1)}, u32[]{:S(2)}) %copy-start.7) | copy-done | bytes 737304
  7.4 0.0 copy-start.8
  7.4 46.8 %exchange.1 = (f32[2,4,16,2880]{3,2,1,0:T(8,128)S(1)}, f32[2,4,16,2880]{3,2,1,0:T(8,128)S(1)}, f32[2,4,16,2880]{3,2,1,0:T(8,128)S(1)}, f32[3,2,16,2880]{3,2,1,0:T(8,128)S(1)}) custom-call(s32[2,32]{1,0:T(2,128)S(1)} %select_reduce_fusion.plan, f32[2,4,16,2880]{3,2,1,0:T(8,128)S(1)} %copy-done, f32[2,4,16,2880]{3,2,1,0:T(8,128)S(1)} %copy-done.1, ...), custom_call_target="tpu_custom_call" | custom-call | tf_op jit(solution)/shard_map/exchange/pallas_call | solution.py:339
  54.3 0.0 copy-done.8
  54.3 0.0 copy-start.3
  54.3 1.1 %copy-done.3 = f32[2,4,16,2880]{3,2,1,0:T(8,128)} copy-done((f32[2,4,16,2880]{3,2,1,0:T(8,128)}, f32[2,4,16,2880]{3,2,1,0:T(8,128)S(1)}, u32[]{:S(2)}) %copy-start.3) | copy-done | bytes 1474584
  55.4 0.0 copy-start.4
  55.4 1.1 %copy-done.4 = f32[2,4,16,2880]{3,2,1,0:T(8,128)} copy-done((f32[2,4,16,2880]{3,2,1,0:T(8,128)}, f32[2,4,16,2880]{3,2,1,0:T(8,128)S(1)}, u32[]{:S(2)}) %copy-start.4) | copy-done | bytes 1474584
  56.6 0.0 copy-start.5
  56.6 1.1 %copy-done.5 = f32[2,4,16,2880]{3,2,1,0:T(8,128)} copy-done((f32[2,4,16,2880]{3,2,1,0:T(8,128)}, f32[2,4,16,2880]{3,2,1,0:T(8,128)S(1)}, u32[]{:S(2)}) %copy-start.5) | copy-done | bytes 1474584
  57.7 0.0 copy-start.6
  57.7 1.0 %copy-done.6 = f32[3,2,16,2880]{3,2,1,0:T(8,128)} copy-done((f32[3,2,16,2880]{3,2,1,0:T(8,128)}, f32[3,2,16,2880]{3,2,1,0:T(8,128)S(1)}, u32[]{:S(2)}) %copy-start.6) | copy-done | bytes 1105944
  58.7 4.9 %place.1 = (f32[2,4,16,2880]{3,2,1,0:T(8,128)}, f32[2,4,16,2880]{3,2,1,0:T(8,128)}, f32[2,4,16,2880]{3,2,1,0:T(8,128)}) custom-call(s32[2,32]{1,0:T(2,128)} %copy-done.8, s32[1]{0:T(128)} %bitcast.mine, f32[2,4,16,2880]{3,2,1,0:T(8,128)} %copy-done.3, f32[2,4,16,2880]{3,2,1,0:T(8,128)} %copy-done.4, f32[2,4,16,2880]{3,2,1,0:T(8,128)} %copy-done.5, ...), custom_call_target="tpu_custom_call" | custom-call | tf_op jit(solution)/shard_map/place/pallas_call | solution.py:405
Async XLA Ops:
  2.2 1.4 %copy-start = (f32[2,4,16,2880]{3,2,1,0:T(8,128)S(1)}, f32[2,4,16,2880]{3,2,1,0:T(8,128)}, u32[]{:S(2)}) copy-start(f32[2,4,16,2880]{3,2,1,0:T(8,128)} %master_hbm.1) | copy-start | bytes 4423684
  3.6 1.4 %copy-start.1 = (f32[2,4,16,2880]{3,2,1,0:T(8,128)S(1)}, f32[2,4,16,2880]{3,2,1,0:T(8,128)}, u32[]{:S(2)}) copy-start(f32[2,4,16,2880]{3,2,1,0:T(8,128)} %one_hbm.1) | copy-start | bytes 4423684
  4.9 1.4 %copy-start.2 = (f32[2,4,16,2880]{3,2,1,0:T(8,128)S(1)}, f32[2,4,16,2880]{3,2,1,0:T(8,128)}, u32[]{:S(2)}) copy-start(f32[2,4,16,2880]{3,2,1,0:T(8,128)} %two_hbm.1) | copy-start | bytes 4423684
  6.3 1.1 %copy-start.7 = (bf16[2,4,16,2880]{3,2,1,0:T(8,128)(2,1)S(1)}, bf16[2,4,16,2880]{3,2,1,0:T(8,128)(2,1)}, u32[]{:S(2)}) copy-start(bf16[2,4,16,2880]{3,2,1,0:T(8,128)(2,1)} %grad_hbm.1) | copy-start | bytes 2211844
  7.4 46.8 %copy-start.8 = (s32[2,32]{1,0:T(2,128)}, s32[2,32]{1,0:T(2,128)S(1)}, u32[]{:S(2)}) copy-start(s32[2,32]{1,0:T(2,128)S(1)} %select_reduce_fusion.plan) | copy-start | bytes 772
  54.3 1.1 %copy-start.3 = (f32[2,4,16,2880]{3,2,1,0:T(8,128)}, f32[2,4,16,2880]{3,2,1,0:T(8,128)S(1)}, u32[]{:S(2)}) copy-start(f32[2,4,16,2880]{3,2,1,0:T(8,128)S(1)} %get-tuple-element.7.w) | copy-start | bytes 4423684
  55.4 1.1 %copy-start.4 = (f32[2,4,16,2880]{3,2,1,0:T(8,128)}, f32[2,4,16,2880]{3,2,1,0:T(8,128)S(1)}, u32[]{:S(2)}) copy-start(f32[2,4,16,2880]{3,2,1,0:T(8,128)S(1)} %get-tuple-element.8.one) | copy-start | bytes 4423684
  56.6 1.1 %copy-start.5 = (f32[2,4,16,2880]{3,2,1,0:T(8,128)}, f32[2,4,16,2880]{3,2,1,0:T(8,128)S(1)}, u32[]{:S(2)}) copy-start(f32[2,4,16,2880]{3,2,1,0:T(8,128)S(1)} %get-tuple-element.9.two) | copy-start | bytes 4423684
  57.7 1.1 %copy-start.6 = (f32[3,2,16,2880]{3,2,1,0:T(8,128)}, f32[3,2,16,2880]{3,2,1,0:T(8,128)S(1)}, u32[]{:S(2)}) copy-start(f32[3,2,16,2880]{3,2,1,0:T(8,128)S(1)} %get-tuple-element.10.landed) | copy-start | bytes 3317764

commit v2 on v1

--- a/solution.py
+++ b/solution.py
@@ -64,15 +64,20 @@
 
 def exchange_kernel(
     entry_count,
-    plan,
     master_hbm,
     one_hbm,
     two_hbm,
     grad_hbm,
+    old_hbm,
+    new_hbm,
     new_w,
     new_one,
     new_two,
     landed,
+    plan,
+    old,
+    new,
+    plan_rows,
     master,
     one,
     two,
@@ -108,7 +113,14 @@
     loads = [
         pltpu.make_async_copy(src, dst, load_sem.at[i])
         for i, (src, dst) in enumerate(
-            ((grad_hbm, grad), (master_hbm, master), (one_hbm, one), (two_hbm, two))
+            (
+                (old_hbm, old),
+                (new_hbm, new),
+                (grad_hbm, grad),
+                (master_hbm, master),
+                (one_hbm, one),
+                (two_hbm, two),
+            )
         )
     ]
     for load in loads:
@@ -121,6 +133,21 @@
         pl.semaphore_signal(barrier, inc=1, device_id={"dp": (dp + d) % DP})
 
     loads[0].wait()
+    loads[1].wait()
+    here = lax.broadcasted_iota(jnp.int32, (GROUP, GROUP * slots), 0)
+    diagonal = lax.broadcasted_iota(jnp.int32, (GROUP, GROUP), 0) == lax.broadcasted_iota(
+        jnp.int32, (GROUP, GROUP), 1
+    )
+    for layer in range(layers):
+        was, now = old[layer : layer + 1], new[layer : layer + 1]
+        word = jnp.where(was != now, (was // slots) * slots + now % slots, 0)
+        word = jnp.where(now // slots == here, word, 0)
+        word = jnp.sum(word, axis=1, keepdims=True)
+        plan_rows[layer : layer + 1] = jnp.sum(jnp.where(diagonal, word, 0), axis=0, keepdims=True)
+    plan_copy = pltpu.make_async_copy(plan_rows, plan, load_sem.at[6])
+    plan_copy.start()
+
+    loads[2].wait()
 
     def square(i, acc):
         for c in range(full):
@@ -137,8 +164,9 @@
     part[...] = acc + jnp.concatenate([tail, jnp.zeros_like(tail)], axis=1)
     parts[pl.ds(me, 1)] = part[...].reshape(1, 1, LANES)
 
-    for load in loads[1:]:
+    for load in loads[3:]:
         load.wait()
+    plan_copy.wait()
 
     my_move = [plan[layer, me] % slots for layer in range(layers)]
 
@@ -329,7 +357,7 @@
     back(back_1, 1, False)
 
 
-def exchange(plan, master, moment_one, moment_two, gradient, entry_count):
+def exchange(master, moment_one, moment_two, gradient, old_slot, new_slot, entry_count):
     layers, slots, rows, cols = master.shape
     vmem = pl.BlockSpec(memory_space=pltpu.VMEM)
     f32 = jnp.float32
@@ -339,10 +367,16 @@
     return pl.pallas_call(
         functools.partial(exchange_kernel, entry_count),
         out_shape=[jax.ShapeDtypeStruct(master.shape, f32)] * 3
-        + [jax.ShapeDtypeStruct((3, layers, rows, cols), f32)],
-        in_specs=[pl.BlockSpec(memory_space=pltpu.SMEM)] + [pl.BlockSpec(memory_space=pl.ANY)] * 4,
-        out_specs=[vmem] * 4,
+        + [
+            jax.ShapeDtypeStruct((3, layers, rows, cols), f32),
+            jax.ShapeDtypeStruct((layers, GROUP), jnp.int32),
+        ],
+        in_specs=[pl.BlockSpec(memory_space=pltpu.HBM)] * 6,
+        out_specs=[vmem] * 4 + [pl.BlockSpec(memory_space=pltpu.SMEM)],
         scratch_shapes=[
+            pltpu.VMEM(old_slot.shape, jnp.int32),
+            pltpu.VMEM(new_slot.shape, jnp.int32),
+            pltpu.VMEM((layers, GROUP), jnp.int32),
             pltpu.VMEM(master.shape, f32),
             pltpu.VMEM(master.shape, f32),
             pltpu.VMEM(master.shape, f32),
@@ -358,7 +392,7 @@
             pltpu.VMEM((GROUP, 1, LANES), f32),
             pltpu.VMEM((1, LANES), f32),
             pltpu.VMEM((DP, 1, LANES), f32),
-            dma((4,)),
+            dma((7,)),
             dma((peers,)),
             dma((peers,)),
             dma((DP - 1,)),
@@ -372,14 +406,19 @@
             collective_id=0, has_side_effects=True, vmem_limit_bytes=40 * 1024 * 1024
         ),
         name="exchange",
-    )(plan, master, moment_one, moment_two, gradient)
-
-
-def place_kernel(plan, mine, w, one, two, landed, out_w, out_one, out_two, sem):
+    )(
+        *(
+            pltpu.with_memory_space_constraint(x, pltpu.HBM)
+            for x in (master, moment_one, moment_two, gradient, old_slot, new_slot)
+        )
+    )
+
+
+def place_kernel(plan, w, one, two, landed, out_w, out_one, out_two, sem):
     layers, slots = w.shape[:2]
     for phase in (0, 1):
         for layer in range(layers):
-            moved = plan[layer, mine[0]] % slots
+            moved = plan[layer, lax.axis_index("expert")] % slots
             for i, (src, dst) in enumerate(((w, out_w), (one, out_one), (two, out_two))):
                 for slot in range(slots):
 
@@ -398,32 +437,26 @@
                         copy.start() if phase == 0 else copy.wait()
 
 
-def place(plan, mine, w, one, two, landed):
+def place(plan, w, one, two, landed):
     layers, slots = w.shape[:2]
-    vmem = pl.BlockSpec(memory_space=pltpu.VMEM)
-    smem = pl.BlockSpec(memory_space=pltpu.SMEM)
     return pl.pallas_call(
         place_kernel,
         out_shape=[jax.ShapeDtypeStruct(w.shape, w.dtype)] * 3,
-        in_specs=[smem, smem] + [vmem] * 4,
+        in_specs=[pl.BlockSpec(memory_space=pltpu.SMEM)] + [pl.BlockSpec(memory_space=pl.ANY)] * 4,
         out_specs=[pl.BlockSpec(memory_space=pl.ANY)] * 3,
         scratch_shapes=[pltpu.SemaphoreType.DMA((3, layers, slots))],
+        compiler_params=pltpu.CompilerParams(vmem_limit_bytes=1024 * 1024),
         name="place",
-    )(plan, mine, w, one, two, landed)
+    )(plan, w, one, two, landed)
 
 
 def shards(master, moment_one, moment_two, gradient, old_slot, new_slot):
     layers, slots, rows, cols = master.shape
     entry_count = layers * slots * GROUP * rows * DP * cols
-    moved = old_slot != new_slot
-    word = (old_slot // slots) * slots + new_slot % slots
-    here = (new_slot // slots)[:, None, :] == lax.broadcasted_iota(
-        jnp.int32, (layers, GROUP, GROUP * slots), 1
+    w, one, two, landed, plan = exchange(
+        master, moment_one, moment_two, gradient, old_slot, new_slot, entry_count
     )
-    plan = jnp.sum(jnp.where(here & moved[:, None, :], word[:, None, :], 0), axis=2)
-    mine = lax.axis_index("expert").reshape(1)
-    w, one, two, landed = exchange(plan, master, moment_one, moment_two, gradient, entry_count)
-    return place(plan, mine, w, one, two, landed)
+    return place(plan, w, one, two, landed)
 
 
 def solution(mesh):

time: 64 us -> 49.2 us (0.77)
  local copies, waits for them, and re-layouts: 9.72 us -> 0 us
  Pallas kernels: 51.8 us -> 48.5 us
  other arithmetic: 1.52 us -> 0 us
    unnamed x18 -> x0, local copies, waits for them, and re-layouts: 9.72 us -> none
    pallas_call x1, Pallas kernels: 4.94 us -> 2.87 us  [place(): pl.pallas_call(place_kernel, out_shape=[jax.ShapeDtypeStruct(w.shape, w.d...]
    pallas_call x1, Pallas kernels: 46.8 us -> 45.6 us  [exchange(): pl.pallas_call(functools.partial(exchange_kernel, entry_count), out_shape...]
    select_n x1 -> x0, other arithmetic: 0.71 us -> none  [shards(): new_slot // slots]
    ne x1 -> x0, other arithmetic: 0.7 us -> none  [shards(): moved = old_slot != new_slot]
where the time goes in v2:
time: 49.2 us; the launch traced here: 49.1 us
  Pallas kernels  48.5 us (99%)
  between operations  0.64 us (1%)
    pallas_call x1, Pallas kernels, exchange(): pl.pallas_call(functools.partial(exchange_kernel, entry_count), out_shape...  45.6 us
    pallas_call x1, Pallas kernels, place(): pl.pallas_call(place_kernel, out_shape=[jax.ShapeDtypeStruct(w.shape, w.d...  2.87 us

profile of v2, /device:TPU:1, one launch (start us, length us, event | category | flops | bytes accessed | tf_op | source)
XLA Modules:
  0.0 49.1 jit_solution(3019963764561921906)
XLA Ops:
  0.6 45.6 %exchange.1 = (f32[2,4,16,2880]{3,2,1,0:T(8,128)S(1)}, f32[2,4,16,2880]{3,2,1,0:T(8,128)S(1)}, f32[2,4,16,2880]{3,2,1,0:T(8,128)S(1)}, f32[3,2,16,2880]{3,2,1,0:T(8,128)S(1)}, s32[2,32]{1,0:T(2,128)S(1)}) custom-call(f32[2,4,16,2880]{3,2,1,0:T(8,128)} %master_hbm.1, f32[2,4,16,2880]{3,2,1,0:T(8,128)} %one_hbm.1, f32[2,4,16,2880]{3,2,1,0:T(8,128)} %two_hbm.1, ...), custom_call_target="tpu_custom_call" | custom-call | tf_op jit(solution)/shard_map/exchange/pallas_call | solution.py:367
  46.3 2.9 %place.1 = (f32[2,4,16,2880]{3,2,1,0:T(8,128)}, f32[2,4,16,2880]{3,2,1,0:T(8,128)}, f32[2,4,16,2880]{3,2,1,0:T(8,128)}) custom-call(s32[2,32]{1,0:T(2,128)S(1)} %get-tuple-element.8.plan, f32[2,4,16,2880]{3,2,1,0:T(8,128)S(1)} %get-tuple-element.9.w, f32[2,4,16,2880]{3,2,1,0:T(8,128)S(1)} %get-tuple-element.10.one, ...), custom_call_target="tpu_custom_call" | custom-call | tf_op jit(solution)/shard_map/place/pallas_call | solution.py:442

commit v3 on v2

v3 whole, which is shorter than its diff:
```python
import functools
import math

import jax
import jax.numpy as jnp
from jax import lax
from jax.experimental import pallas as pl
from jax.experimental.pallas import tpu as pltpu
from jax.sharding import PartitionSpec as P

BETA_ONE = 0.9
BETA_TWO = 0.95
LEARN_RATE = 0.05
DECAY_RATE = 0.1
ADAM_EPS = 1e-08
CLIP_RMS = 2.0
FIRST_FIX = 1.0 - 0.9**10
SECOND_FIX = 1.0 - 0.95**10

ZDIM, YDIM, CORES = 4, 4, 2
GROUP = ZDIM * YDIM * CORES
DP = 4
LANES = 128
SUB = 4
PIECE = 3
UNITS = 90


def move_order():
    moves = [
        (dz, dy, dc)
        for dz in (0, 1, 2, -1)
        for dy in (0, 1, 2, -1)
        for dc in (0, 1)
        if (dz, dy, dc) != (0, 0, 0)
    ]
    neg = lambda v: v if v == 2 else -v
    order = []
    for dz, dy, dc in sorted(moves, key=lambda m: -(abs(m[0]) + abs(m[1]))):
        for m in ((dz, dy, dc), (neg(dz), neg(dy), dc), (dy, dz, dc), (neg(dy), neg(dz), dc)):
            if m not in order:
                order.append(m)
    return order


MOVES = move_order()


def shifted(me, move):
    dz, dy, dc = move
    core, y, z = me % CORES, (me // CORES) % YDIM, me // (CORES * YDIM)
    z = (z + dz + ZDIM) % ZDIM
    y = (y + dy + YDIM) % YDIM
    return (z * YDIM + y) * CORES + (core + dc) % CORES


def adam(master, moment_one, moment_two, gradient, scale):
    scaled = gradient * scale
    first = BETA_ONE * moment_one + (1.0 - BETA_ONE) * scaled
    second = BETA_TWO * moment_two + (1.0 - BETA_TWO) * scaled * scaled
    step = (first * (1.0 / FIRST_FIX)) / (jnp.sqrt(second * (1.0 / SECOND_FIX)) + ADAM_EPS)
    return master - LEARN_RATE * (step + DECAY_RATE * master), first, second


def is_short(layer, holder):
    return holder % 5 == (4, 2)[layer]


def offset(layer, holder):
    return PIECE * holder - (holder + (0, 2)[layer]) // 5


def unpack(home, block):
    _, rows, cols = block.shape
    full = cols // LANES
    width = cols - full * LANES
    for i in range(block.shape[0]):
        for c in range(full):
            x = home[4 * c : 4 * c + 4, i]
            block[i, :, c * LANES : (c + 1) * LANES] = x.reshape(rows, LANES)
        x = home[4 * full : 4 * full + 2, i]
        x = jnp.stack([x[:, :, :width], x[:, :, width:]], axis=1)
        block[i, :, full * LANES :] = x.reshape(rows, width)


def exchange_kernel(
    entry_count,
    master_hbm,
    one_hbm,
    two_hbm,
    grad_hbm,
    old_hbm,
    new_hbm,
    new_w,
    new_one,
    new_two,
    landed,
    home_1,
    plan,
    old,
    new,
    plan_rows,
    master,
    one,
    two,
    grad,
    send_raw,
    send_new,
    hold_raw,
    hold_new,
    back_0,
    back_1,
    home_0,
    part,
    parts,
    line,
    lines,
    load_sem,
    part_sem,
    out_sem,
    back_sem,
):
    layers, slots, rows, cols = master.shape
    full = cols // LANES
    dp = lax.axis_index("dp")
    me = lax.axis_index("expert")
    targets = [shifted(me, m) for m in MOVES]
    home_of = (home_0, home_1)

    loads = [
        pltpu.make_async_copy(src, dst, load_sem.at[i])
        for i, (src, dst) in enumerate(
            (
                (old_hbm, old),
                (new_hbm, new),
                (grad_hbm, grad),
                (master_hbm, master),
                (one_hbm, one),
                (two_hbm, two),
            )
        )
    ]
    for load in loads:
        load.start()

    barrier = pltpu.get_barrier_semaphore()
    for t in targets:
        pl.semaphore_signal(barrier, inc=1, device_id={"expert": t})
    for d in range(1, DP):
        pl.semaphore_signal(barrier, inc=1, device_id={"dp": (dp + d) % DP})

    loads[0].wait()
    loads[1].wait()
    here = lax.broadcasted_iota(jnp.int32, (GROUP, GROUP * slots), 0)
    diagonal = lax.broadcasted_iota(jnp.int32, (GROUP, GROUP), 0) == lax.broadcasted_iota(
        jnp.int32, (GROUP, GROUP), 1
    )
    for layer in range(layers):
        was, now = old[layer : layer + 1], new[layer : layer + 1]
        word = jnp.where(was != now, (was // slots) * slots + now % slots, 0)
        word = jnp.where(now // slots == here, word, 0)
        word = jnp.sum(word, axis=1, keepdims=True)
        plan_rows[layer : layer + 1] = jnp.sum(jnp.where(diagonal, word, 0), axis=0, keepdims=True)
    plan_copy = pltpu.make_async_copy(plan_rows, plan, load_sem.at[6])
    plan_copy.start()

    loads[2].wait()

    def square(i, acc):
        for c in range(full):
            g = grad[i // slots, i % slots, :, c * LANES : (c + 1) * LANES].astype(jnp.float32)
            acc = acc + g * g
        return acc

    acc = lax.fori_loop(
        0, layers * slots, square, jnp.zeros((rows, LANES), jnp.float32)
    )
    tail = grad[:, :, :, full * LANES :].astype(jnp.float32)
    tail = jnp.sum((tail * tail).reshape(layers * slots * rows, cols - full * LANES), axis=0, keepdims=True)
    acc = jnp.sum(acc, axis=0, keepdims=True)
    part[...] = acc + jnp.concatenate([tail, jnp.zeros_like(tail)], axis=1)
    parts[pl.ds(me, 1)] = part[...].reshape(1, 1, LANES)

    for load in loads[3:]:
        load.wait()
    plan_copy.wait()

    my_move = [plan[layer, me] % slots for layer in range(layers)]

    def units(x):
        return x.reshape(rows // SUB, SUB, LANES)

    def joined(x):
        x = x.reshape(rows // SUB // 2, 2, SUB, cols - full * LANES)
        return jnp.concatenate([x[:, 0], x[:, 1]], axis=-1)

    for i, ref in enumerate((master, one, two, grad)):
        for c in range(full):
            x = ref[0, my_move[0], :, c * LANES : (c + 1) * LANES].astype(jnp.float32)
            send_raw[4 * c : 4 * c + 4, i] = units(x)
        x = ref[0, my_move[0], :, full * LANES :].astype(jnp.float32)
        send_raw[4 * full : 4 * full + 2, i] = joined(x)

    pl.semaphore_wait(barrier, len(MOVES) + DP - 1)

    for t in targets:
        pltpu.make_async_remote_copy(
            part, parts.at[me], part_sem.at[0], part_sem.at[1], device_id={"expert": t}
        ).start()

    def bytes_of(ref, sem):
        return pltpu.make_async_copy(ref, ref, sem)

    def sized(layer, holder, body):
        short = is_short(layer, holder)

        @pl.when(short)
        def _():
            body(PIECE - 1)

        @pl.when(jnp.logical_not(short))
        def _():
            body(PIECE)

    def out(send, hold, layer):
        for t in targets:

            def start(size):
                pltpu.make_async_remote_copy(
                    send.at[pl.ds(offset(layer, t), size)],
                    hold.at[me, pl.ds(0, size)],
                    out_sem.at[layer, 0],
                    out_sem.at[layer, 1],
                    device_id={"expert": t},
                ).start()

            sized(layer, t, start)

        def keep(size):
            hold[pl.ds(me, 1), 0:size] = send[pl.ds(offset(layer, me), size)][None]

        sized(layer, me, keep)

    def arrived(hold, layer):
        def wait(size):
            bytes_of(hold.at[0 : GROUP - 1, 0:size], out_sem.at[layer, 1]).wait()

        sized(layer, me, wait)

    def back(buf, layer):
        def start(size):
            for t in targets:
                pltpu.make_async_remote_copy(
                    buf.at[t, pl.ds(0, size)],
                    home_of[layer].at[pl.ds(offset(layer, me), size)],
                    back_sem.at[layer, 0],
                    back_sem.at[layer, 1],
                    device_id={"expert": t},
                ).start()
            home_of[layer][pl.ds(offset(layer, me), size)] = buf[me, 0:size]

        sized(layer, me, start)

    def returned(layer):
        def wait(size):
            bytes_of(home_of[layer].at[0 : UNITS - size], back_sem.at[layer, 1]).wait()

        sized(layer, me, wait)

    def sent(send, buf, layer):
        def wait(size):
            bytes_of(send.at[0 : UNITS - size], out_sem.at[layer, 0]).wait()
            bytes_of(buf.at[0 : GROUP - 1, 0:size], back_sem.at[layer, 0]).wait()

        sized(layer, me, wait)

    out(send_raw, hold_raw, 0)

    bytes_of(parts.at[0 : GROUP - 1], part_sem.at[1]).wait()
    plane = jnp.sum(parts[...].reshape(GROUP, LANES), axis=0, keepdims=True)
    line[...] = plane
    lines[pl.ds(dp, 1)] = plane.reshape(1, 1, LANES)
    for d in range(1, DP):
        pltpu.make_async_remote_copy(
            line, lines.at[dp], part_sem.at[2], part_sem.at[3], device_id={"dp": (dp + d) % DP}
        ).start()
    bytes_of(lines.at[0 : DP - 1], part_sem.at[3]).wait()
    total = jnp.sum(lines[...].reshape(DP, LANES), axis=0, keepdims=True)
    total = jnp.sum(total, axis=1, keepdims=True)
    scale = jnp.minimum(1.0, CLIP_RMS * math.sqrt(entry_count) / (jnp.sqrt(total) + 1e-06))

    for c in range(full):
        at = (1, my_move[1], slice(None), slice(c * LANES, (c + 1) * LANES))
        done = adam(master[at], one[at], two[at], grad[at].astype(jnp.float32), scale)
        for i, x in enumerate(done):
            send_new[4 * c : 4 * c + 4, i] = units(x)
    at = (1, my_move[1], slice(None), slice(full * LANES, cols))
    done = adam(master[at], one[at], two[at], grad[at].astype(jnp.float32), scale)
    for i, x in enumerate(done):
        send_new[4 * full : 4 * full + 2, i] = joined(x)
    out(send_new, hold_new, 1)

    def resident(i, _):
        layer, slot = i // slots, i % slots
        for lo in range(0, cols, 2 * LANES):
            at = (layer, slot, slice(None), slice(lo, min(lo + 2 * LANES, cols)))
            done = adam(master[at], one[at], two[at], grad[at].astype(jnp.float32), scale)
            for ref, x in zip((new_w, new_one, new_two), done):
                ref[at] = x
        return 0

    lax.fori_loop(0, layers * slots, resident, 0)

    arrived(hold_raw, 0)

    def forward_raw(t, _):
        x = hold_raw[plan[0, t] // slots]
        done = adam(x[:, 0], x[:, 1], x[:, 2], x[:, 3], scale)
        for i, y in enumerate(done):
            back_0[t, :, i] = y
        return 0

    lax.fori_loop(0, GROUP, forward_raw, 0)
    back(back_0, 0)

    arrived(hold_new, 1)

    def forward_new(t, _):
        back_1[t] = hold_new[plan[1, t] // slots]
        return 0

    lax.fori_loop(0, GROUP, forward_new, 0)
    back(back_1, 1)

    returned(0)
    unpack(home_0, landed)
    returned(1)

    bytes_of(parts.at[0 : GROUP - 1], part_sem.at[0]).wait()
    bytes_of(lines.at[0 : DP - 1], part_sem.at[2]).wait()
    sent(send_raw, back_0, 0)
    sent(send_new, back_1, 1)


def exchange(master, moment_one, moment_two, gradient, old_slot, new_slot, entry_count):
    layers, slots, rows, cols = master.shape
    vmem = pl.BlockSpec(memory_space=pltpu.VMEM)
    f32 = jnp.float32
    dma = pltpu.SemaphoreType.DMA
    return pl.pallas_call(
        functools.partial(exchange_kernel, entry_count),
        out_shape=[jax.ShapeDtypeStruct(master.shape, f32)] * 3
        + [
            jax.ShapeDtypeStruct((3, rows, cols), f32),
            jax.ShapeDtypeStruct((UNITS, 3, SUB, LANES), f32),
            jax.ShapeDtypeStruct((layers, GROUP), jnp.int32),
        ],
        in_specs=[pl.BlockSpec(memory_space=pltpu.HBM)] * 6,
        out_specs=[vmem] * 5 + [pl.BlockSpec(memory_space=pltpu.SMEM)],
        scratch_shapes=[
            pltpu.VMEM(old_slot.shape, jnp.int32),
            pltpu.VMEM(new_slot.shape, jnp.int32),
            pltpu.VMEM((layers, GROUP), jnp.int32),
            pltpu.VMEM(master.shape, f32),
            pltpu.VMEM(master.shape, f32),
            pltpu.VMEM(master.shape, f32),
            pltpu.VMEM(master.shape, jnp.bfloat16),
            pltpu.VMEM((UNITS, 4, SUB, LANES), f32),
            pltpu.VMEM((UNITS, 3, SUB, LANES), f32),
            pltpu.VMEM((GROUP, PIECE, 4, SUB, LANES), f32),
            pltpu.VMEM((GROUP, PIECE, 3, SUB, LANES), f32),
            pltpu.VMEM((GROUP, PIECE, 3, SUB, LANES), f32),
            pltpu.VMEM((GROUP, PIECE, 3, SUB, LANES), f32),
            pltpu.VMEM((UNITS, 3, SUB, LANES), f32),
            pltpu.VMEM((1, LANES), f32),
            pltpu.VMEM((GROUP, 1, LANES), f32),
            pltpu.VMEM((1, LANES), f32),
            pltpu.VMEM((DP, 1, LANES), f32),
            dma((7,)),
            dma((4,)),
            dma((layers, 2)),
            dma((layers, 2)),
        ],
        compiler_params=pltpu.CompilerParams(
            collective_id=0, has_side_effects=True, vmem_limit_bytes=40 * 1024 * 1024
        ),
        name="exchange",
    )(
        *(
            pltpu.with_memory_space_constraint(x, pltpu.HBM)
            for x in (master, moment_one, moment_two, gradient, old_slot, new_slot)
        )
    )


def place_kernel(plan, w, one, two, landed, home, out_w, out_one, out_two, last, sem):
    layers, slots = w.shape[:2]
    pairs = ((w, out_w), (one, out_one), (two, out_two))
    moved = [plan[layer, lax.axis_index("expert")] % slots for layer in range(layers)]
    for layer in range(layers):
        for i, (src, dst) in enumerate(pairs):
            for slot in range(slots):

                @pl.when(slot != moved[layer])
                def _():
                    pltpu.make_async_copy(
                        src.at[layer, slot], dst.at[layer, slot], sem.at[i]
                    ).start()

    unpack(home, last)
    for layer, block in enumerate((landed, last)):
        for i, (_, dst) in enumerate(pairs):
            pltpu.make_async_copy(block.at[i], dst.at[layer, moved[layer]], sem.at[i]).start()
    for i, (src, dst) in enumerate(pairs):
        pltpu.make_async_copy(src, dst, sem.at[i]).wait()


def place(plan, w, one, two, landed, home):
    rows, cols = w.shape[2:]
    vmem = pl.BlockSpec(memory_space=pltpu.VMEM)
    free = pl.BlockSpec(memory_space=pl.ANY)
    return pl.pallas_call(
        place_kernel,
        out_shape=[jax.ShapeDtypeStruct(w.shape, w.dtype)] * 3,
        in_specs=[pl.BlockSpec(memory_space=pltpu.SMEM)] + [free] * 4 + [vmem],
        out_specs=[free] * 3,
        scratch_shapes=[pltpu.VMEM((3, rows, cols), w.dtype), pltpu.SemaphoreType.DMA((3,))],
        compiler_params=pltpu.CompilerParams(vmem_limit_bytes=4 * 1024 * 1024),
        name="place",
    )(plan, w, one, two, landed, home)


def shards(master, moment_one, moment_two, gradient, old_slot, new_slot):
    layers, slots, rows, cols = master.shape
    entry_count = layers * slots * GROUP * rows * DP * cols
    w, one, two, landed, home, plan = exchange(
        master, moment_one, moment_two, gradient, old_slot, new_slot, entry_count
    )
    return place(plan, w, one, two, landed, home)


def solution(mesh):
    spec = P(None, "expert", "dp", None)
    return jax.shard_map(
        shards,
        mesh=mesh,
        in_specs=(spec, spec, spec, spec, P(), P()),
        out_specs=(spec, spec, spec),
        check_vma=False,
    )
```

time: 49.2 us -> 43.2 us (0.88); the launches traced: 49.1 us -> 42.5 us
  Pallas kernels: 48.5 us -> 41.9 us
    pallas_call x1, Pallas kernels: 45.6 us -> 39.2 us  [exchange(): pl.pallas_call(functools.partial(exchange_kernel, entry_count), out_shape...]
where the time goes in v3:
time: 43.2 us; the launch traced here: 42.5 us
  Pallas kernels  41.9 us (97%)
  between operations  0.64 us (1%)
    pallas_call x1, Pallas kernels, exchange(): pl.pallas_call(functools.partial(exchange_kernel, entry_count), out_shape...  39.2 us
    pallas_call x1, Pallas kernels, place(): pl.pallas_call(place_kernel, out_shape=[jax.ShapeDtypeStruct(w.shape, w.d...  2.68 us

profile of v3, /device:TPU:1, one launch (start us, length us, event | category | flops | bytes accessed | tf_op | source)
XLA Modules:
  0.0 42.5 jit_solution(4546572970126190403)
XLA Ops:
  0.6 39.2 %exchange.1 = (f32[2,4,16,2880]{3,2,1,0:T(8,128)S(1)}, f32[2,4,16,2880]{3,2,1,0:T(8,128)S(1)}, f32[2,4,16,2880]{3,2,1,0:T(8,128)S(1)}, f32[3,16,2880]{2,1,0:T(8,...) custom-call(f32[2,4,16,2880]{3,2,1,0:T(8,128)} %master_hbm.1, f32[2,4,16,2880]{3,2,1,0:T(8,128)} %one_hbm.1, ...), custom_call_target="tpu_custom_call" | custom-call | tf_op jit(solution)/shard_map/exchange/pallas_call | solution.py:350
  39.9 2.7 %place.1 = (f32[2,4,16,2880]{3,2,1,0:T(8,128)}, f32[2,4,16,2880]{3,2,1,0:T(8,128)}, f32[2,4,16,2880]{3,2,1,0:T(8,128)}) custom-call(s32[2,32]{1,0:T(2,128)S(1)} %get-tuple-element.9.plan, f32[2,4,16,2880]{3,2,1,0:T(8,128)S(1)} %get-tuple-element.10.w, f32[2,4,16,2880]{3,2,1,0:T(8,128)S(1)} %get-tuple-element.11.one, ...), custom_call_target="tpu_custom_call" | custom-call | tf_op jit(solution)/shard_map/place/pallas_call | solution.py:422

commit v4 on v3

--- a/solution.py
+++ b/solution.py
@@ -24,6 +24,7 @@
 SUB = 4
 PIECE = 3
 UNITS = 90
+CHAINS = 6
 
 
 def move_order():
@@ -96,13 +97,16 @@
     new_two,
     landed,
     home_1,
-    plan,
+    plan_rows,
     old,
     new,
-    plan_rows,
-    master,
-    one,
-    two,
+    plan,
+    master_0,
+    master_1,
+    one_0,
+    one_1,
+    two_0,
+    two_1,
     grad,
     send_raw,
     send_new,
@@ -120,28 +124,14 @@
     out_sem,
     back_sem,
 ):
-    layers, slots, rows, cols = master.shape
+    layers, slots, rows, cols = master_hbm.shape
+    master, one, two = (master_0, master_1), (one_0, one_1), (two_0, two_1)
     full = cols // LANES
     dp = lax.axis_index("dp")
     me = lax.axis_index("expert")
     targets = [shifted(me, m) for m in MOVES]
+    orders = (targets[-9:-1] + targets[:-9] + targets[-1:], targets)
     home_of = (home_0, home_1)
-
-    loads = [
-        pltpu.make_async_copy(src, dst, load_sem.at[i])
-        for i, (src, dst) in enumerate(
-            (
-                (old_hbm, old),
-                (new_hbm, new),
-                (grad_hbm, grad),
-                (master_hbm, master),
-                (one_hbm, one),
-                (two_hbm, two),
-            )
-        )
-    ]
-    for load in loads:
-        load.start()
 
     barrier = pltpu.get_barrier_semaphore()
     for t in targets:
@@ -149,8 +139,21 @@
     for d in range(1, DP):
         pl.semaphore_signal(barrier, inc=1, device_id={"dp": (dp + d) % DP})
 
-    loads[0].wait()
-    loads[1].wait()
+    def load(src, dst, sem):
+        copy = pltpu.make_async_copy(src, dst, load_sem.at[sem])
+        copy.start()
+        return copy
+
+    old_load, new_load = load(old_hbm, old, 0), load(new_hbm, new, 1)
+    grad_load = load(grad_hbm, grad, 2)
+    arrays = ((master_hbm, master), (one_hbm, one), (two_hbm, two))
+    loads = [
+        [load(src.at[layer], dst[layer], 3 + 3 * layer + i) for i, (src, dst) in enumerate(arrays)]
+        for layer in range(layers)
+    ]
+
+    old_load.wait()
+    new_load.wait()
     here = lax.broadcasted_iota(jnp.int32, (GROUP, GROUP * slots), 0)
     diagonal = lax.broadcasted_iota(jnp.int32, (GROUP, GROUP), 0) == lax.broadcasted_iota(
         jnp.int32, (GROUP, GROUP), 1
@@ -161,46 +164,26 @@
         word = jnp.where(now // slots == here, word, 0)
         word = jnp.sum(word, axis=1, keepdims=True)
         plan_rows[layer : layer + 1] = jnp.sum(jnp.where(diagonal, word, 0), axis=0, keepdims=True)
-    plan_copy = pltpu.make_async_copy(plan_rows, plan, load_sem.at[6])
+    plan_copy = pltpu.make_async_copy(plan_rows, plan, load_sem.at[9])
     plan_copy.start()
 
-    loads[2].wait()
-
-    def square(i, acc):
+    grad_load.wait()
+
+    def square(i, accs):
+        accs = list(accs)
         for c in range(full):
             g = grad[i // slots, i % slots, :, c * LANES : (c + 1) * LANES].astype(jnp.float32)
-            acc = acc + g * g
-        return acc
-
-    acc = lax.fori_loop(
-        0, layers * slots, square, jnp.zeros((rows, LANES), jnp.float32)
-    )
+            accs[c % CHAINS] += g * g
+        return tuple(accs)
+
+    zero = jnp.zeros((rows, LANES), jnp.float32)
+    acc = sum(lax.fori_loop(0, layers * slots, square, (zero,) * CHAINS))
     tail = grad[:, :, :, full * LANES :].astype(jnp.float32)
     tail = jnp.sum((tail * tail).reshape(layers * slots * rows, cols - full * LANES), axis=0, keepdims=True)
     acc = jnp.sum(acc, axis=0, keepdims=True)
     part[...] = acc + jnp.concatenate([tail, jnp.zeros_like(tail)], axis=1)
     parts[pl.ds(me, 1)] = part[...].reshape(1, 1, LANES)
 
-    for load in loads[3:]:
-        load.wait()
-    plan_copy.wait()
-
-    my_move = [plan[layer, me] % slots for layer in range(layers)]
-
-    def units(x):
-        return x.reshape(rows // SUB, SUB, LANES)
-
-    def joined(x):
-        x = x.reshape(rows // SUB // 2, 2, SUB, cols - full * LANES)
-        return jnp.concatenate([x[:, 0], x[:, 1]], axis=-1)
-
-    for i, ref in enumerate((master, one, two, grad)):
-        for c in range(full):
-            x = ref[0, my_move[0], :, c * LANES : (c + 1) * LANES].astype(jnp.float32)
-            send_raw[4 * c : 4 * c + 4, i] = units(x)
-        x = ref[0, my_move[0], :, full * LANES :].astype(jnp.float32)
-        send_raw[4 * full : 4 * full + 2, i] = joined(x)
-
     pl.semaphore_wait(barrier, len(MOVES) + DP - 1)
 
     for t in targets:
@@ -208,6 +191,26 @@
             part, parts.at[me], part_sem.at[0], part_sem.at[1], device_id={"expert": t}
         ).start()
 
+    for copy in loads[0]:
+        copy.wait()
+    plan_copy.wait()
+
+    my_move = [plan[layer, me] % slots for layer in range(layers)]
+
+    def units(x):
+        return x.reshape(rows // SUB, SUB, LANES)
+
+    def joined(x):
+        x = x.reshape(rows // SUB // 2, 2, SUB, cols - full * LANES)
+        return jnp.concatenate([x[:, 0], x[:, 1]], axis=-1)
+
+    for i, ref in enumerate((master_0, one_0, two_0, grad.at[0])):
+        for c in range(full):
+            x = ref[my_move[0], :, c * LANES : (c + 1) * LANES].astype(jnp.float32)
+            send_raw[4 * c : 4 * c + 4, i] = units(x)
+        x = ref[my_move[0], :, full * LANES :].astype(jnp.float32)
+        send_raw[4 * full : 4 * full + 2, i] = joined(x)
+
     def bytes_of(ref, sem):
         return pltpu.make_async_copy(ref, ref, sem)
 
@@ -223,7 +226,7 @@
             body(PIECE)
 
     def out(send, hold, layer):
-        for t in targets:
+        for t in orders[layer]:
 
             def start(size):
                 pltpu.make_async_remote_copy(
@@ -236,10 +239,11 @@
 
             sized(layer, t, start)
 
-        def keep(size):
+    def keep(send, hold, layer):
+        def body(size):
             hold[pl.ds(me, 1), 0:size] = send[pl.ds(offset(layer, me), size)][None]
 
-        sized(layer, me, keep)
+        sized(layer, me, body)
 
     def arrived(hold, layer):
         def wait(size):
@@ -275,41 +279,40 @@
         sized(layer, me, wait)
 
     out(send_raw, hold_raw, 0)
+    for copy in loads[1]:
+        copy.wait()
 
     bytes_of(parts.at[0 : GROUP - 1], part_sem.at[1]).wait()
-    plane = jnp.sum(parts[...].reshape(GROUP, LANES), axis=0, keepdims=True)
-    line[...] = plane
-    lines[pl.ds(dp, 1)] = plane.reshape(1, 1, LANES)
+    line[...] = jnp.sum(parts[...].reshape(GROUP, LANES), axis=0, keepdims=True)
+    lines[pl.ds(dp, 1)] = line[...].reshape(1, 1, LANES)
     for d in range(1, DP):
         pltpu.make_async_remote_copy(
             line, lines.at[dp], part_sem.at[2], part_sem.at[3], device_id={"dp": (dp + d) % DP}
         ).start()
+    keep(send_raw, hold_raw, 0)
     bytes_of(lines.at[0 : DP - 1], part_sem.at[3]).wait()
     total = jnp.sum(lines[...].reshape(DP, LANES), axis=0, keepdims=True)
     total = jnp.sum(total, axis=1, keepdims=True)
     scale = jnp.minimum(1.0, CLIP_RMS * math.sqrt(entry_count) / (jnp.sqrt(total) + 1e-06))
 
+    def updated(layer, at):
+        return adam(
+            master[layer][at],
+            one[layer][at],
+            two[layer][at],
+            grad[(layer, *at)].astype(jnp.float32),
+            scale,
+        )
+
     for c in range(full):
-        at = (1, my_move[1], slice(None), slice(c * LANES, (c + 1) * LANES))
-        done = adam(master[at], one[at], two[at], grad[at].astype(jnp.float32), scale)
+        done = updated(1, (my_move[1], slice(None), slice(c * LANES, (c + 1) * LANES)))
         for i, x in enumerate(done):
             send_new[4 * c : 4 * c + 4, i] = units(x)
-    at = (1, my_move[1], slice(None), slice(full * LANES, cols))
-    done = adam(master[at], one[at], two[at], grad[at].astype(jnp.float32), scale)
+    done = updated(1, (my_move[1], slice(None), slice(full * LANES, cols)))
     for i, x in enumerate(done):
         send_new[4 * full : 4 * full + 2, i] = joined(x)
     out(send_new, hold_new, 1)
-
-    def resident(i, _):
-        layer, slot = i // slots, i % slots
-        for lo in range(0, cols, 2 * LANES):
-            at = (layer, slot, slice(None), slice(lo, min(lo + 2 * LANES, cols)))
-            done = adam(master[at], one[at], two[at], grad[at].astype(jnp.float32), scale)
-            for ref, x in zip((new_w, new_one, new_two), done):
-                ref[at] = x
-        return 0
-
-    lax.fori_loop(0, layers * slots, resident, 0)
+    keep(send_new, hold_new, 1)
 
     arrived(hold_raw, 0)
 
@@ -322,6 +325,17 @@
 
     lax.fori_loop(0, GROUP, forward_raw, 0)
     back(back_0, 0)
+
+    for layer in range(layers):
+
+        def resident(slot, _):
+            for lo in range(0, cols, 2 * LANES):
+                at = (slot, slice(None), slice(lo, min(lo + 2 * LANES, cols)))
+                for ref, x in zip((new_w, new_one, new_two), updated(layer, at)):
+                    ref[(layer, *at)] = x
+            return 0
+
+        lax.fori_loop(0, slots, resident, 0)
 
     arrived(hold_new, 1)
 
@@ -356,14 +370,12 @@
             jax.ShapeDtypeStruct((layers, GROUP), jnp.int32),
         ],
         in_specs=[pl.BlockSpec(memory_space=pltpu.HBM)] * 6,
-        out_specs=[vmem] * 5 + [pl.BlockSpec(memory_space=pltpu.SMEM)],
+        out_specs=[vmem] * 6,
         scratch_shapes=[
             pltpu.VMEM(old_slot.shape, jnp.int32),
             pltpu.VMEM(new_slot.shape, jnp.int32),
-            pltpu.VMEM((layers, GROUP), jnp.int32),
-            pltpu.VMEM(master.shape, f32),
-            pltpu.VMEM(master.shape, f32),
-            pltpu.VMEM(master.shape, f32),
+            pltpu.SMEM((layers, GROUP), jnp.int32),
+            *[pltpu.VMEM(master.shape[1:], f32)] * (3 * layers),
             pltpu.VMEM(master.shape, jnp.bfloat16),
             pltpu.VMEM((UNITS, 4, SUB, LANES), f32),
             pltpu.VMEM((UNITS, 3, SUB, LANES), f32),
@@ -376,7 +388,7 @@
             pltpu.VMEM((GROUP, 1, LANES), f32),
             pltpu.VMEM((1, LANES), f32),
             pltpu.VMEM((DP, 1, LANES), f32),
-            dma((7,)),
+            dma((10,)),
             dma((4,)),
             dma((layers, 2)),
             dma((layers, 2)),
@@ -396,7 +408,9 @@
 def place_kernel(plan, w, one, two, landed, home, out_w, out_one, out_two, last, sem):
     layers, slots = w.shape[:2]
     pairs = ((w, out_w), (one, out_one), (two, out_two))
-    moved = [plan[layer, lax.axis_index("expert")] % slots for layer in range(layers)]
+    mine = lax.broadcasted_iota(jnp.int32, plan.shape, 1) == lax.axis_index("expert")
+    chosen = jnp.where(mine, plan[...], 0)
+    moved = [jnp.sum(chosen[layer : layer + 1]) % slots for layer in range(layers)]
     for layer in range(layers):
         for i, (src, dst) in enumerate(pairs):
             for slot in range(slots):
@@ -422,7 +436,7 @@
     return pl.pallas_call(
         place_kernel,
         out_shape=[jax.ShapeDtypeStruct(w.shape, w.dtype)] * 3,
-        in_specs=[pl.BlockSpec(memory_space=pltpu.SMEM)] + [free] * 4 + [vmem],
+        in_specs=[vmem] + [free] * 4 + [vmem],
         out_specs=[free] * 3,
         scratch_shapes=[pltpu.VMEM((3, rows, cols), w.dtype), pltpu.SemaphoreType.DMA((3,))],
         compiler_params=pltpu.CompilerParams(vmem_limit_bytes=4 * 1024 * 1024),

time: 43.2 us -> 41.5 us (0.961)
  Pallas kernels: 41.9 us -> 40.4 us
    pallas_call x1, Pallas kernels: 39.2 us -> 38.2 us  [exchange(): pl.pallas_call(functools.partial(exchange_kernel, entry_count), out_shape...]
where the time goes in v4:
time: 41.5 us; the launch traced here: 41.1 us
  Pallas kernels  40.4 us (97%)
  between operations  0.64 us (2%)
    pallas_call x1, Pallas kernels, exchange(): pl.pallas_call(functools.partial(exchange_kernel, entry_count), out_shape...  38.2 us
    pallas_call x1, Pallas kernels, place(): pl.pallas_call(place_kernel, out_shape=[jax.ShapeDtypeStruct(w.shape, w.d...  2.26 us

profile of v4, /device:TPU:1, one launch (start us, length us, event | category | flops | bytes accessed | tf_op | source)
XLA Modules:
  0.0 41.1 jit_solution(837430427868053048)
XLA Ops:
  0.6 38.2 %exchange.1 = (f32[2,4,16,2880]{3,2,1,0:T(8,128)S(1)}, f32[2,4,16,2880]{3,2,1,0:T(8,128)S(1)}, f32[2,4,16,2880]{3,2,1,0:T(8,128)S(1)}, f32[3,16,2880]{2,1,0:T(8,...) custom-call(f32[2,4,16,2880]{3,2,1,0:T(8,128)} %master_hbm.1, f32[2,4,16,2880]{3,2,1,0:T(8,128)} %one_hbm.1, ...), custom_call_target="tpu_custom_call" | custom-call | tf_op jit(solution)/shard_map/exchange/pallas_call | solution.py:364
  38.8 2.3 %place.1 = (f32[2,4,16,2880]{3,2,1,0:T(8,128)}, f32[2,4,16,2880]{3,2,1,0:T(8,128)}, f32[2,4,16,2880]{3,2,1,0:T(8,128)}) custom-call(s32[2,32]{1,0:T(2,128)S(1)} %get-tuple-element.9.plan, f32[2,4,16,2880]{3,2,1,0:T(8,128)S(1)} %get-tuple-element.10.w, f32[2,4,16,2880]{3,2,1,0:T(8,128)S(1)} %get-tuple-element.11.one, ...), custom_call_target="tpu_custom_call" | custom-call | tf_op jit(solution)/shard_map/place/pallas_call | solution.py:436

commit v5 on v4

--- a/solution.py
+++ b/solution.py
@@ -23,6 +23,7 @@
 LANES = 128
 SUB = 4
 PIECE = 3
+RAW = 2
 UNITS = 90
 CHAINS = 6
 
@@ -55,12 +56,21 @@
     return (z * YDIM + y) * CORES + (core + dc) % CORES
 
 
-def adam(master, moment_one, moment_two, gradient, scale):
+def moments(moment_one, moment_two, gradient, scale):
     scaled = gradient * scale
     first = BETA_ONE * moment_one + (1.0 - BETA_ONE) * scaled
     second = BETA_TWO * moment_two + (1.0 - BETA_TWO) * scaled * scaled
+    return first, second
+
+
+def stepped(master, first, second):
     step = (first * (1.0 / FIRST_FIX)) / (jnp.sqrt(second * (1.0 / SECOND_FIX)) + ADAM_EPS)
-    return master - LEARN_RATE * (step + DECAY_RATE * master), first, second
+    return master - LEARN_RATE * (step + DECAY_RATE * master)
+
+
+def adam(master, moment_one, moment_two, gradient, scale):
+    first, second = moments(moment_one, moment_two, gradient, scale)
+    return stepped(master, first, second), first, second
 
 
 def is_short(layer, holder):
@@ -109,10 +119,15 @@
     two_1,
     grad,
     send_raw,
+    send_master,
+    send_rest,
     send_new,
     hold_raw,
+    hold_master,
+    hold_rest,
     hold_new,
     back_0,
+    back_rest,
     back_1,
     home_0,
     part,
@@ -130,8 +145,7 @@
     dp = lax.axis_index("dp")
     me = lax.axis_index("expert")
     targets = [shifted(me, m) for m in MOVES]
-    orders = (targets[-9:-1] + targets[:-9] + targets[-1:], targets)
-    home_of = (home_0, home_1)
+    near_first = targets[-9:-1] + targets[:-9] + targets[-1:]
 
     barrier = pltpu.get_barrier_semaphore()
     for t in targets:
@@ -225,62 +239,65 @@
         def _():
             body(PIECE)
 
-    def out(send, hold, layer):
-        for t in orders[layer]:
+    def post(src, dst, batch, t):
+        pltpu.make_async_remote_copy(
+            src, dst, out_sem.at[batch, 0], out_sem.at[batch, 1], device_id={"expert": t}
+        ).start()
+
+    def out(send, hold, layer, batch):
+        for t in targets:
 
             def start(size):
-                pltpu.make_async_remote_copy(
-                    send.at[pl.ds(offset(layer, t), size)],
-                    hold.at[me, pl.ds(0, size)],
-                    out_sem.at[layer, 0],
-                    out_sem.at[layer, 1],
-                    device_id={"expert": t},
-                ).start()
+                src = send.at[pl.ds(offset(layer, t), size)]
+                post(src, hold.at[me, pl.ds(0, size)], batch, t)
 
             sized(layer, t, start)
 
-    def keep(send, hold, layer):
-        def body(size):
+        def keep(size):
             hold[pl.ds(me, 1), 0:size] = send[pl.ds(offset(layer, me), size)][None]
 
-        sized(layer, me, body)
-
-    def arrived(hold, layer):
+        sized(layer, me, keep)
+
+    def arrived(hold, layer, batch):
         def wait(size):
-            bytes_of(hold.at[0 : GROUP - 1, 0:size], out_sem.at[layer, 1]).wait()
+            bytes_of(hold.at[0 : GROUP - 1, 0:size], out_sem.at[batch, 1]).wait()
 
         sized(layer, me, wait)
 
-    def back(buf, layer):
-        def start(size):
-            for t in targets:
-                pltpu.make_async_remote_copy(
-                    buf.at[t, pl.ds(0, size)],
-                    home_of[layer].at[pl.ds(offset(layer, me), size)],
-                    back_sem.at[layer, 0],
-                    back_sem.at[layer, 1],
-                    device_id={"expert": t},
-                ).start()
-            home_of[layer][pl.ds(offset(layer, me), size)] = buf[me, 0:size]
-
-        sized(layer, me, start)
-
-    def returned(layer):
+    def sent(send, layer, batch):
         def wait(size):
-            bytes_of(home_of[layer].at[0 : UNITS - size], back_sem.at[layer, 1]).wait()
+            bytes_of(send.at[0 : UNITS - size], out_sem.at[batch, 0]).wait()
 
         sized(layer, me, wait)
 
-    def sent(send, buf, layer):
-        def wait(size):
-            bytes_of(send.at[0 : UNITS - size], out_sem.at[layer, 0]).wait()
-            bytes_of(buf.at[0 : GROUP - 1, 0:size], back_sem.at[layer, 0]).wait()
-
-        sized(layer, me, wait)
-
-    out(send_raw, hold_raw, 0)
+    def reply(src, dst, batch, t):
+        pltpu.make_async_remote_copy(
+            src, dst, back_sem.at[batch, 0], back_sem.at[batch, 1], device_id={"expert": t}
+        ).start()
+
+    def other_whole(body):
+        whole = GROUP - sum(is_short(0, holder) for holder in range(GROUP))
+        short = is_short(0, me)
+
+        @pl.when(short)
+        def _():
+            body(whole)
+
+        @pl.when(jnp.logical_not(short))
+        def _():
+            body(whole - 1)
+
+    for t in near_first:
+        post(send_raw.at[pl.ds(offset(0, t), RAW)], hold_raw.at[me], 0, t)
+    hold_raw[pl.ds(me, 1)] = send_raw[pl.ds(offset(0, me), RAW)][None]
     for copy in loads[1]:
         copy.wait()
+
+    for c in range(full):
+        x = master_1[my_move[1], :, c * LANES : (c + 1) * LANES]
+        send_master[4 * c : 4 * c + 4] = units(x)
+    send_master[4 * full : 4 * full + 2] = joined(master_1[my_move[1], :, full * LANES :])
+    out(send_master, hold_master, 1, 1)
 
     bytes_of(parts.at[0 : GROUP - 1], part_sem.at[1]).wait()
     line[...] = jnp.sum(parts[...].reshape(GROUP, LANES), axis=0, keepdims=True)
@@ -289,71 +306,120 @@
         pltpu.make_async_remote_copy(
             line, lines.at[dp], part_sem.at[2], part_sem.at[3], device_id={"dp": (dp + d) % DP}
         ).start()
-    keep(send_raw, hold_raw, 0)
     bytes_of(lines.at[0 : DP - 1], part_sem.at[3]).wait()
     total = jnp.sum(lines[...].reshape(DP, LANES), axis=0, keepdims=True)
     total = jnp.sum(total, axis=1, keepdims=True)
     scale = jnp.minimum(1.0, CLIP_RMS * math.sqrt(entry_count) / (jnp.sqrt(total) + 1e-06))
 
-    def updated(layer, at):
-        return adam(
+    for holder in range(GROUP):
+        if not is_short(0, holder):
+            x = send_raw[offset(0, holder) + RAW]
+            for i, y in enumerate(adam(x[0], x[1], x[2], x[3], scale)):
+                send_rest[holder, i] = y
+    for t in targets:
+
+        @pl.when(jnp.logical_not(is_short(0, t)))
+        def _():
+            post(send_rest.at[t], hold_rest.at[me], 2, t)
+
+    hold_rest[pl.ds(me, 1)] = send_rest[pl.ds(me, 1)]
+
+    def inputs(layer, at):
+        return (
             master[layer][at],
             one[layer][at],
             two[layer][at],
             grad[(layer, *at)].astype(jnp.float32),
-            scale,
         )
 
     for c in range(full):
-        done = updated(1, (my_move[1], slice(None), slice(c * LANES, (c + 1) * LANES)))
-        for i, x in enumerate(done):
+        at = (my_move[1], slice(None), slice(c * LANES, (c + 1) * LANES))
+        for i, x in enumerate(moments(*inputs(1, at)[1:], scale)):
             send_new[4 * c : 4 * c + 4, i] = units(x)
-    done = updated(1, (my_move[1], slice(None), slice(full * LANES, cols)))
-    for i, x in enumerate(done):
+    at = (my_move[1], slice(None), slice(full * LANES, cols))
+    for i, x in enumerate(moments(*inputs(1, at)[1:], scale)):
         send_new[4 * full : 4 * full + 2, i] = joined(x)
-    out(send_new, hold_new, 1)
-    keep(send_new, hold_new, 1)
-
-    arrived(hold_raw, 0)
+    out(send_new, hold_new, 1, 3)
+
+    bytes_of(hold_raw.at[0 : GROUP - 1], out_sem.at[0, 1]).wait()
 
     def forward_raw(t, _):
-        x = hold_raw[plan[0, t] // slots]
-        done = adam(x[:, 0], x[:, 1], x[:, 2], x[:, 3], scale)
-        for i, y in enumerate(done):
+        source = plan[0, t] // slots
+        x = hold_raw[source]
+        for i, y in enumerate(adam(x[:, 0], x[:, 1], x[:, 2], x[:, 3], scale)):
             back_0[t, :, i] = y
         return 0
 
     lax.fori_loop(0, GROUP, forward_raw, 0)
-    back(back_0, 0)
+    here = pl.ds(offset(0, me), RAW)
+    for t in targets:
+        reply(back_0.at[t], home_0.at[here], 0, t)
+    home_0[here] = back_0[me]
 
     for layer in range(layers):
 
         def resident(slot, _):
             for lo in range(0, cols, 2 * LANES):
                 at = (slot, slice(None), slice(lo, min(lo + 2 * LANES, cols)))
-                for ref, x in zip((new_w, new_one, new_two), updated(layer, at)):
+                for ref, x in zip((new_w, new_one, new_two), adam(*inputs(layer, at), scale)):
                     ref[(layer, *at)] = x
             return 0
 
         lax.fori_loop(0, slots, resident, 0)
 
-    arrived(hold_new, 1)
+    @pl.when(jnp.logical_not(is_short(0, me)))
+    def _():
+        bytes_of(hold_rest.at[0 : GROUP - 1], out_sem.at[2, 1]).wait()
+
+        def forward_rest(t, _):
+            back_rest[t] = hold_rest[plan[0, t] // slots]
+            return 0
+
+        lax.fori_loop(0, GROUP, forward_rest, 0)
+        for t in targets:
+            reply(back_rest.at[t], home_0.at[offset(0, me) + RAW], 1, t)
+        home_0[pl.ds(offset(0, me) + RAW, 1)] = back_rest[pl.ds(me, 1)]
+
+    arrived(hold_master, 1, 1)
+    arrived(hold_new, 1, 3)
 
     def forward_new(t, _):
-        back_1[t] = hold_new[plan[1, t] // slots]
+        source = plan[1, t] // slots
+        x = hold_new[source]
+        back_1[t, :, 0] = stepped(hold_master[source], x[:, 0], x[:, 1])
+        back_1[t, :, 1:3] = x
         return 0
 
     lax.fori_loop(0, GROUP, forward_new, 0)
-    back(back_1, 1)
-
-    returned(0)
+
+    def send_back(size):
+        at = pl.ds(offset(1, me), size)
+        for t in targets:
+            reply(back_1.at[t, pl.ds(0, size)], home_1.at[at], 2, t)
+        home_1[at] = back_1[me, 0:size]
+
+    sized(1, me, send_back)
+
+    bytes_of(home_0.at[0 : RAW * (GROUP - 1)], back_sem.at[0, 1]).wait()
+    other_whole(lambda count: bytes_of(home_0.at[0:count], back_sem.at[1, 1]).wait())
     unpack(home_0, landed)
-    returned(1)
+    sized(1, me, lambda size: bytes_of(home_1.at[0 : UNITS - size], back_sem.at[2, 1]).wait())
 
     bytes_of(parts.at[0 : GROUP - 1], part_sem.at[0]).wait()
     bytes_of(lines.at[0 : DP - 1], part_sem.at[2]).wait()
-    sent(send_raw, back_0, 0)
-    sent(send_new, back_1, 1)
+    bytes_of(send_raw.at[0 : RAW * (GROUP - 1)], out_sem.at[0, 0]).wait()
+    sent(send_master, 1, 1)
+    other_whole(lambda count: bytes_of(send_rest.at[0:count], out_sem.at[2, 0]).wait())
+    sent(send_new, 1, 3)
+    bytes_of(back_0.at[0 : GROUP - 1], back_sem.at[0, 0]).wait()
+
+    @pl.when(jnp.logical_not(is_short(0, me)))
+    def _():
+        bytes_of(back_rest.at[0 : GROUP - 1], back_sem.at[1, 0]).wait()
+
+    sized(
+        1, me, lambda size: bytes_of(back_1.at[0 : GROUP - 1, 0:size], back_sem.at[2, 0]).wait()
+    )
 
 
 def exchange(master, moment_one, moment_two, gradient, old_slot, new_slot, entry_count):
@@ -378,10 +444,15 @@
             *[pltpu.VMEM(master.shape[1:], f32)] * (3 * layers),
             pltpu.VMEM(master.shape, jnp.bfloat16),
             pltpu.VMEM((UNITS, 4, SUB, LANES), f32),
-            pltpu.VMEM((UNITS, 3, SUB, LANES), f32),
-            pltpu.VMEM((GROUP, PIECE, 4, SUB, LANES), f32),
-            pltpu.VMEM((GROUP, PIECE, 3, SUB, LANES), f32),
-            pltpu.VMEM((GROUP, PIECE, 3, SUB, LANES), f32),
+            pltpu.VMEM((UNITS, SUB, LANES), f32),
+            pltpu.VMEM((GROUP, 3, SUB, LANES), f32),
+            pltpu.VMEM((UNITS, 2, SUB, LANES), f32),
+            pltpu.VMEM((GROUP, RAW, 4, SUB, LANES), f32),
+            pltpu.VMEM((GROUP, PIECE, SUB, LANES), f32),
+            pltpu.VMEM((GROUP, 3, SUB, LANES), f32),
+            pltpu.VMEM((GROUP, PIECE, 2, SUB, LANES), f32),
+            pltpu.VMEM((GROUP, RAW, 3, SUB, LANES), f32),
+            pltpu.VMEM((GROUP, 3, SUB, LANES), f32),
             pltpu.VMEM((GROUP, PIECE, 3, SUB, LANES), f32),
             pltpu.VMEM((UNITS, 3, SUB, LANES), f32),
             pltpu.VMEM((1, LANES), f32),
@@ -390,8 +461,8 @@
             pltpu.VMEM((DP, 1, LANES), f32),
             dma((10,)),
             dma((4,)),
-            dma((layers, 2)),
-            dma((layers, 2)),
+            dma((4, 2)),
+            dma((3, 2)),
         ],
         compiler_params=pltpu.CompilerParams(
             collective_id=0, has_side_effects=True, vmem_limit_bytes=40 * 1024 * 1024

time: 41.5 us -> 40.5 us (0.976)
  Pallas kernels: 40.4 us -> 39.5 us
    pallas_call x1, Pallas kernels: 38.2 us -> 37.3 us  [exchange(): pl.pallas_call(functools.partial(exchange_kernel, entry_count), out_shape...]
where the time goes in v5:
time: 40.5 us; the launch traced here: 40.2 us
  Pallas kernels  39.5 us (98%)
  between operations  0.64 us (2%)
    pallas_call x1, Pallas kernels, exchange(): pl.pallas_call(functools.partial(exchange_kernel, entry_count), out_shape...  37.3 us
    pallas_call x1, Pallas kernels, place(): pl.pallas_call(place_kernel, out_shape=[jax.ShapeDtypeStruct(w.shape, w.d...  2.26 us

profile of v5, /device:TPU:1, one launch (start us, length us, event | category | flops | bytes accessed | tf_op | source)
XLA Modules:
  0.0 40.2 jit_solution(3302078473024115044)
XLA Ops:
  0.6 37.3 %exchange.1 = (f32[2,4,16,2880]{3,2,1,0:T(8,128)S(1)}, f32[2,4,16,2880]{3,2,1,0:T(8,128)S(1)}, f32[2,4,16,2880]{3,2,1,0:T(8,128)S(1)}, f32[3,16,2880]{2,1,0:T(8,...) custom-call(f32[2,4,16,2880]{3,2,1,0:T(8,128)} %master_hbm.1, f32[2,4,16,2880]{3,2,1,0:T(8,128)} %one_hbm.1, ...), custom_call_target="tpu_custom_call" | custom-call | tf_op jit(solution)/shard_map/exchange/pallas_call | solution.py:430
  37.9 2.3 %place.1 = (f32[2,4,16,2880]{3,2,1,0:T(8,128)}, f32[2,4,16,2880]{3,2,1,0:T(8,128)}, f32[2,4,16,2880]{3,2,1,0:T(8,128)}) custom-call(s32[2,32]{1,0:T(2,128)S(1)} %get-tuple-element.9.plan, f32[2,4,16,2880]{3,2,1,0:T(8,128)S(1)} %get-tuple-element.10.w, f32[2,4,16,2880]{3,2,1,0:T(8,128)S(1)} %get-tuple-element.11.one, ...), custom_call_target="tpu_custom_call" | custom-call | tf_op jit(solution)/shard_map/place/pallas_call | solution.py:507

commit v6 on v5

--- a/solution.py
+++ b/solution.py
@@ -25,6 +25,7 @@
 PIECE = 3
 RAW = 2
 UNITS = 90
+BATCH = 8
 CHAINS = 6
 
 
@@ -161,10 +162,10 @@
     old_load, new_load = load(old_hbm, old, 0), load(new_hbm, new, 1)
     grad_load = load(grad_hbm, grad, 2)
     arrays = ((master_hbm, master), (one_hbm, one), (two_hbm, two))
-    loads = [
-        [load(src.at[layer], dst[layer], 3 + 3 * layer + i) for i, (src, dst) in enumerate(arrays)]
-        for layer in range(layers)
-    ]
+    def load_layer(layer):
+        return [load(src.at[layer], dst[layer], 3 + 3 * layer + i) for i, (src, dst) in enumerate(arrays)]
+
+    loads = [load_layer(0)]
 
     old_load.wait()
     new_load.wait()
@@ -198,6 +199,7 @@
     part[...] = acc + jnp.concatenate([tail, jnp.zeros_like(tail)], axis=1)
     parts[pl.ds(me, 1)] = part[...].reshape(1, 1, LANES)
 
+    loads.append(load_layer(1))
     pl.semaphore_wait(barrier, len(MOVES) + DP - 1)
 
     for t in targets:
@@ -356,6 +358,47 @@
         reply(back_0.at[t], home_0.at[here], 0, t)
     home_0[here] = back_0[me]
 
+    @pl.when(jnp.logical_not(is_short(0, me)))
+    def _():
+        bytes_of(hold_rest.at[0 : GROUP - 1], out_sem.at[2, 1]).wait()
+
+        def forward_rest(t, _):
+            back_rest[t] = hold_rest[plan[0, t] // slots]
+            return 0
+
+        lax.fori_loop(0, GROUP, forward_rest, 0)
+        for t in targets:
+            reply(back_rest.at[t], home_0.at[offset(0, me) + RAW], 1, t)
+        home_0[pl.ds(offset(0, me) + RAW, 1)] = back_rest[pl.ds(me, 1)]
+
+    arrived(hold_master, 1, 1)
+    arrived(hold_new, 1, 3)
+
+    def forward_new(t):
+        source = plan[1, t] // slots
+        x = hold_new[source]
+        back_1[t, :, 0] = stepped(hold_master[source], x[:, 0], x[:, 1])
+        back_1[t, :, 1:3] = x
+
+    def send_back(some):
+        def start(size):
+            for t in some:
+                src = back_1.at[t, pl.ds(0, size)]
+                reply(src, home_1.at[pl.ds(offset(1, me), size)], 2, t)
+
+        sized(1, me, start)
+
+    groups = [targets[k : k + BATCH] for k in range(0, len(targets), BATCH)]
+    for some, before in zip(groups + [[me]], [[]] + groups):
+        for t in some:
+            forward_new(t)
+        send_back(before)
+
+    def keep_back(size):
+        home_1[pl.ds(offset(1, me), size)] = back_1[me, 0:size]
+
+    sized(1, me, keep_back)
+
     for layer in range(layers):
 
         def resident(slot, _):
@@ -366,39 +409,6 @@
             return 0
 
         lax.fori_loop(0, slots, resident, 0)
-
-    @pl.when(jnp.logical_not(is_short(0, me)))
-    def _():
-        bytes_of(hold_rest.at[0 : GROUP - 1], out_sem.at[2, 1]).wait()
-
-        def forward_rest(t, _):
-            back_rest[t] = hold_rest[plan[0, t] // slots]
-            return 0
-
-        lax.fori_loop(0, GROUP, forward_rest, 0)
-        for t in targets:
-            reply(back_rest.at[t], home_0.at[offset(0, me) + RAW], 1, t)
-        home_0[pl.ds(offset(0, me) + RAW, 1)] = back_rest[pl.ds(me, 1)]
-
-    arrived(hold_master, 1, 1)
-    arrived(hold_new, 1, 3)
-
-    def forward_new(t, _):
-        source = plan[1, t] // slots
-        x = hold_new[source]
-        back_1[t, :, 0] = stepped(hold_master[source], x[:, 0], x[:, 1])
-        back_1[t, :, 1:3] = x
-        return 0
-
-    lax.fori_loop(0, GROUP, forward_new, 0)
-
-    def send_back(size):
-        at = pl.ds(offset(1, me), size)
-        for t in targets:
-            reply(back_1.at[t, pl.ds(0, size)], home_1.at[at], 2, t)
-        home_1[at] = back_1[me, 0:size]
-
-    sized(1, me, send_back)
 
     bytes_of(home_0.at[0 : RAW * (GROUP - 1)], back_sem.at[0, 1]).wait()
     other_whole(lambda count: bytes_of(home_0.at[0:count], back_sem.at[1, 1]).wait())

time: 40.5 us -> 40.2 us (level)
  no operation moved by 1% of the time
where the time goes in v6:
time: 40.2 us; the launch traced here: 40.1 us
  Pallas kernels  39.5 us (98%)
  between operations  0.64 us (2%)
    pallas_call x1, Pallas kernels, exchange(): pl.pallas_call(functools.partial(exchange_kernel, entry_count), out_shape...  37.2 us
    pallas_call x1, Pallas kernels, place(): pl.pallas_call(place_kernel, out_shape=[jax.ShapeDtypeStruct(w.shape, w.d...  2.26 us

profile of v6, /device:TPU:1, one launch (start us, length us, event | category | flops | bytes accessed | tf_op | source)
XLA Modules:
  0.0 40.1 jit_solution(13613330055749014349)
XLA Ops:
  0.6 37.2 %exchange.1 = (f32[2,4,16,2880]{3,2,1,0:T(8,128)S(1)}, f32[2,4,16,2880]{3,2,1,0:T(8,128)S(1)}, f32[2,4,16,2880]{3,2,1,0:T(8,128)S(1)}, f32[3,16,2880]{2,1,0:T(8,...) custom-call(f32[2,4,16,2880]{3,2,1,0:T(8,128)} %master_hbm.1, f32[2,4,16,2880]{3,2,1,0:T(8,128)} %one_hbm.1, ...), custom_call_target="tpu_custom_call" | custom-call | tf_op jit(solution)/shard_map/exchange/pallas_call | solution.py:440
  37.9 2.3 %place.1 = (f32[2,4,16,2880]{3,2,1,0:T(8,128)}, f32[2,4,16,2880]{3,2,1,0:T(8,128)}, f32[2,4,16,2880]{3,2,1,0:T(8,128)}) custom-call(s32[2,32]{1,0:T(2,128)S(1)} %get-tuple-element.9.plan, f32[2,4,16,2880]{3,2,1,0:T(8,128)S(1)} %get-tuple-element.10.w, f32[2,4,16,2880]{3,2,1,0:T(8,128)S(1)} %get-tuple-element.11.one, ...), custom_call_target="tpu_custom_call" | custom-call | tf_op jit(solution)/shard_map/place/pallas_call | solution.py:517

commit v7 on v6

--- a/solution.py
+++ b/solution.py
@@ -345,17 +345,18 @@
 
     bytes_of(hold_raw.at[0 : GROUP - 1], out_sem.at[0, 1]).wait()
 
-    def forward_raw(t, _):
-        source = plan[0, t] // slots
-        x = hold_raw[source]
+    def forward_raw(t):
+        x = hold_raw[plan[0, t] // slots]
         for i, y in enumerate(adam(x[:, 0], x[:, 1], x[:, 2], x[:, 3], scale)):
             back_0[t, :, i] = y
-        return 0
-
-    lax.fori_loop(0, GROUP, forward_raw, 0)
+
     here = pl.ds(offset(0, me), RAW)
-    for t in targets:
-        reply(back_0.at[t], home_0.at[here], 0, t)
+    groups = [targets[k : k + BATCH] for k in range(0, len(targets), BATCH)]
+    for some, before in zip(groups + [[me]], [[]] + groups):
+        for t in some:
+            forward_raw(t)
+        for t in before:
+            reply(back_0.at[t], home_0.at[here], 0, t)
     home_0[here] = back_0[me]
 
     @pl.when(jnp.logical_not(is_short(0, me)))
@@ -388,7 +389,6 @@
 
         sized(1, me, start)
 
-    groups = [targets[k : k + BATCH] for k in range(0, len(targets), BATCH)]
     for some, before in zip(groups + [[me]], [[]] + groups):
         for t in some:
             forward_new(t)

time: 40.2 us -> 40.2 us (level)
  no operation moved by 1% of the time
where the time goes in v7:
time: 40.2 us; the launch traced here: 40.1 us
  Pallas kernels  39.5 us (98%)
  between operations  0.64 us (2%)
    pallas_call x1, Pallas kernels, exchange(): pl.pallas_call(functools.partial(exchange_kernel, entry_count), out_shape...  37.2 us
    pallas_call x1, Pallas kernels, place(): pl.pallas_call(place_kernel, out_shape=[jax.ShapeDtypeStruct(w.shape, w.d...  2.26 us

profile of v7, /device:TPU:1, one launch (start us, length us, event | category | flops | bytes accessed | tf_op | source)
XLA Modules:
  0.0 40.1 jit_solution(3725103979853698823)
XLA Ops:
  0.6 37.2 %exchange.1 = (f32[2,4,16,2880]{3,2,1,0:T(8,128)S(1)}, f32[2,4,16,2880]{3,2,1,0:T(8,128)S(1)}, f32[2,4,16,2880]{3,2,1,0:T(8,128)S(1)}, f32[3,16,2880]{2,1,0:T(8,...) custom-call(f32[2,4,16,2880]{3,2,1,0:T(8,128)} %master_hbm.1, f32[2,4,16,2880]{3,2,1,0:T(8,128)} %one_hbm.1, ...), custom_call_target="tpu_custom_call" | custom-call | tf_op jit(solution)/shard_map/exchange/pallas_call | solution.py:440
  37.9 2.3 %place.1 = (f32[2,4,16,2880]{3,2,1,0:T(8,128)}, f32[2,4,16,2880]{3,2,1,0:T(8,128)}, f32[2,4,16,2880]{3,2,1,0:T(8,128)}) custom-call(s32[2,32]{1,0:T(2,128)S(1)} %get-tuple-element.9.plan, f32[2,4,16,2880]{3,2,1,0:T(8,128)S(1)} %get-tuple-element.10.w, f32[2,4,16,2880]{3,2,1,0:T(8,128)S(1)} %get-tuple-element.11.one, ...), custom_call_target="tpu_custom_call" | custom-call | tf_op jit(solution)/shard_map/place/pallas_call | solution.py:517

commit v8 on v6

--- a/solution.py
+++ b/solution.py
@@ -25,7 +25,7 @@
 PIECE = 3
 RAW = 2
 UNITS = 90
-BATCH = 8
+BATCH = 16
 CHAINS = 6
 
 

time: 40.2 us -> 40.1 us (level)
  no operation moved by 1% of the time
where the time goes in v8:
time: 40.1 us; the launch traced here: 40 us
  Pallas kernels  39.4 us (98%)
  between operations  0.64 us (2%)
    pallas_call x1, Pallas kernels, exchange(): pl.pallas_call(functools.partial(exchange_kernel, entry_count), out_shape...  37.1 us
    pallas_call x1, Pallas kernels, place(): pl.pallas_call(place_kernel, out_shape=[jax.ShapeDtypeStruct(w.shape, w.d...  2.26 us

profile of v8, /device:TPU:1, one launch (start us, length us, event | category | flops | bytes accessed | tf_op | source)
XLA Modules:
  0.0 40.0 jit_solution(4542110028351763050)
XLA Ops:
  0.6 37.1 %exchange.1 = (f32[2,4,16,2880]{3,2,1,0:T(8,128)S(1)}, f32[2,4,16,2880]{3,2,1,0:T(8,128)S(1)}, f32[2,4,16,2880]{3,2,1,0:T(8,128)S(1)}, f32[3,16,2880]{2,1,0:T(8,...) custom-call(f32[2,4,16,2880]{3,2,1,0:T(8,128)} %master_hbm.1, f32[2,4,16,2880]{3,2,1,0:T(8,128)} %one_hbm.1, ...), custom_call_target="tpu_custom_call" | custom-call | tf_op jit(solution)/shard_map/exchange/pallas_call | solution.py:440
  37.8 2.3 %place.1 = (f32[2,4,16,2880]{3,2,1,0:T(8,128)}, f32[2,4,16,2880]{3,2,1,0:T(8,128)}, f32[2,4,16,2880]{3,2,1,0:T(8,128)}) custom-call(s32[2,32]{1,0:T(2,128)S(1)} %get-tuple-element.9.plan, f32[2,4,16,2880]{3,2,1,0:T(8,128)S(1)} %get-tuple-element.10.w, f32[2,4,16,2880]{3,2,1,0:T(8,128)S(1)} %get-tuple-element.11.one, ...), custom_call_target="tpu_custom_call" | custom-call | tf_op jit(solution)/shard_map/place/pallas_call | solution.py:517
